TPU v7x, 32 devices: a whole 2x2x4 slice. The times are simulated.
32 devices in a mesh: dp: 8 (over z, x), tensor: 4 (over y, core).
Axes of the slice: x: 2, y: 2, z: 4, core: 2. Of those that a mesh axis runs over, the one named last changes fastest.
Arguments:
- tokens: bfloat16 [2, 8, 1024, 1024], P(None, 'dp', 'tensor'), may hold values from -6 to 6
- segment_ids: int32 [2, 8, 1024], P(None, 'dp'), may hold values from 0 to 2, as said below
- attn_gain: float32 [1024], replicated, may hold values from 0.1 to 1.9
- query_gain: float32 [64], replicated, may hold values from 0.1 to 1.9
- key_gain: float32 [64], replicated, may hold values from 0.1 to 1.9
- w_query: bfloat16 [1024, 1024], P('dp', 'tensor'), may hold values from -0.1875 to 0.1875
- w_key: bfloat16 [1024, 512], P('dp', 'tensor'), may hold values from -0.1875 to 0.1875
- w_value: bfloat16 [1024, 512], P('dp', 'tensor'), may hold values from -0.1875 to 0.1875
- w_out: bfloat16 [1024, 1024], P('tensor', 'dp'), may hold values from -1.5 to 1.5
- ffn_gain: float32 [1024], replicated, may hold values from 0.1 to 1.9
- w_gate: bfloat16 [1024, 4608], P('dp', 'tensor'), may hold values from -0.1875 to 0.1875
- w_up: bfloat16 [1024, 4608], P('dp', 'tensor'), may hold values from -0.1875 to 0.1875
- w_down: bfloat16 [4608, 1024], P('tensor', 'dp'), may hold values from -0.09375 to 0.09375
- cotangent: bfloat16 [2, 8, 1024, 1024], P(None, 'dp', 'tensor'), may hold values from -6 to 6
Outputs:
- mixed: bfloat16 [2, 8, 1024, 1024], P(None, 'dp', 'tensor')
- grad_tokens: float32 [2, 8, 1024, 1024], P(None, 'dp', 'tensor')
- grad_attn_gain: float32 [1024], replicated
- grad_query_gain: float32 [64], replicated
- grad_key_gain: float32 [64], replicated
- grad_query: float32 [1024, 1024], P('dp', 'tensor')
- grad_key: float32 [1024, 512], P('dp', 'tensor')
- grad_value: float32 [1024, 512], P('dp', 'tensor')
- grad_out: float32 [1024, 1024], P('tensor', 'dp')
- grad_ffn_gain: float32 [1024], replicated
- grad_gate: float32 [1024, 4608], P('dp', 'tensor')
- grad_up: float32 [1024, 4608], P('dp', 'tensor')
- grad_down: float32 [4608, 1024], P('tensor', 'dp')
Inputs may be any that keep to these rules, and one draw needn't show every extreme that they name: `segment_ids`: ids never fall along a sequence and every sequence holds documents 0, 1 and 2; document 0 has 204 to 408 tokens, document 1 has 204 to 511 tokens.
All inputs are finite; a program needn't handle non-finite values.
Results may differ from a plain program's by a relative error of at most 0.017.
Values may be sent and summed in bfloat16 or wider, within the bound.
A program may use at most 112 MiB of HBM per device.

v0:
```python
import functools
import math

import jax
import jax.numpy as jnp
import numpy as np
from jax import lax
from jax.experimental import pallas as pl
from jax.experimental.pallas import tpu as pltpu
from jax.sharding import PartitionSpec as P

MESH = pl.DeviceIdType.MESH
VMEM_LIMIT = 67000000
NORM_EPS = 1e-05
ROPE_BASE = 1000000.0
DH = 64
TILE = 256
LN2 = math.log(2.0)
APART = -32768.0
BF16 = jnp.bfloat16
F32 = jnp.float32


def nn(left, right):
    return lax.dot_general(left, right, (((1,), (0,)), ((), ())), preferred_element_type=F32)


def nt(left, right):
    return lax.dot_general(left, right, (((1,), (1,)), ((), ())), preferred_element_type=F32)


def tn(left, right):
    return lax.dot_general(left, right, (((0,), (0,)), ((), ())), preferred_element_type=F32)


def tile(index, size=TILE):
    return pl.ds(pl.multiple_of(index * size, size), size)


def rem(value, divisor):
    return value % divisor if isinstance(value, int) else lax.rem(value, divisor)


def low_parts(values):
    high = values.astype(BF16)
    return high, (values - high.astype(F32)).astype(BF16)


def head_mean(values, mixer):
    high, rest = low_parts(values)
    return nn(high, mixer) + nn(rest, mixer)


def swap_halves(values):
    lane = lax.broadcasted_iota(jnp.int32, values.shape, 1)
    ahead = pltpu.roll(values, 96, 1)
    behind = pltpu.roll(values, 32, 1)
    return jnp.where(lax.rem(lane, 64) < 32, ahead, behind)


def norm_rows(values, gain):
    inverse = lax.rsqrt(jnp.mean(values * values, axis=-1, keepdims=True) + NORM_EPS)
    return values * inverse * gain


def norm_rows_back(values, gain, upstream):
    inverse = lax.rsqrt(jnp.mean(values * values, axis=-1, keepdims=True) + NORM_EPS)
    scaled = values * inverse
    weighted = upstream * gain
    back = inverse * (weighted - scaled * jnp.mean(weighted * scaled, axis=-1, keepdims=True))
    return back, jnp.sum(upstream * scaled, axis=0, keepdims=True)


class Place:
    def __init__(self, dp_size):
        self.dp_size = dp_size
        self.dp = lax.axis_index("dp")
        self.tensor = lax.axis_index("tensor")
        self.outer_size = dp_size // 2
        self.outer = self.dp // 2
        self.inner = lax.rem(self.dp, 2)
        self.other = self.outer * 2 + 1 - self.inner
        self.side = self.tensor // 2
        self.core = lax.rem(self.tensor, 2)
        self.across = (1 - self.side) * 2 + self.core
        self.twin = self.side * 2 + 1 - self.core

    def ahead(self, shift, inner=None):
        inner = self.inner if inner is None else inner
        return lax.rem(self.outer + shift, self.outer_size) * 2 + inner

    def behind(self, shift):
        return lax.rem(self.outer - shift + self.outer_size, self.outer_size) * 2 + self.inner

    def block(self, step):
        side = 1 - self.side if step < 2 else self.side
        core = 1 - self.core if step % 2 == 0 else self.core
        return side * 2 + core

    def copy(self, src, dst, sems, index, dp=None, tensor=None):
        return pltpu.make_async_remote_copy(
            src_ref=src,
            dst_ref=dst,
            send_sem=sems[0].at[index],
            recv_sem=sems[1].at[index],
            device_id=(
                self.dp if dp is None else dp,
                self.tensor if tensor is None else tensor,
            ),
            device_id_type=MESH,
        )

    def greet(self, everyone):
        barrier = pltpu.get_barrier_semaphore()

        def signal(dp, tensor):
            pl.semaphore_signal(barrier, inc=1, device_id=(dp, tensor), device_id_type=MESH)

        if everyone:

            @pl.loop(1, self.dp_size)
            def _(shift):
                signal(lax.rem(self.dp + shift, self.dp_size), self.tensor)

            for shift in range(1, 4):
                signal(self.dp, lax.rem(self.tensor + shift, 4))
            pl.semaphore_wait(barrier, self.dp_size + 2)
        else:

            @pl.loop(1, self.outer_size)
            def _(shift):
                signal(self.ahead(shift), self.tensor)

            signal(self.other, self.tensor)
            signal(self.dp, self.across)
            signal(self.dp, self.twin)
            pl.semaphore_wait(barrier, self.outer_size + 2)


def pack_gains(packed, terms):
    part = 0
    for row, width in enumerate((terms.shape[1], terms.shape[1], 256)):
        for start in range(0, width, 128):
            packed[part // 3 : part // 3 + 1, 128 * (part % 3) : 128 * (part % 3) + 128] = terms[
                row : row + 1, start : start + 128
            ]
            part += 1


class Gather:
    def __init__(self, place, ref, micro, sems, index, source=None):
        own = ref.at[micro, tile(place.tensor)]
        source = own if source is None else source
        theirs = ref.at[micro, tile(place.across)]
        self.to_across = place.copy(source, own, sems, index, tensor=place.across)
        self.to_twin = place.copy(source, own, sems, index + 1, tensor=place.twin)
        self.on_to_twin = place.copy(theirs, theirs, sems, index + 2, tensor=place.twin)

    def start(self):
        self.to_across.start()
        self.to_twin.start()

    def relay(self):
        self.to_across.wait_recv()
        self.on_to_twin.start()

    def finish(self):
        self.to_twin.wait_recv()
        self.on_to_twin.wait_recv()

    def drain(self):
        self.to_across.wait_send()
        self.to_twin.wait_send()
        self.on_to_twin.wait_send()


class Scatter:
    def __init__(self, place, staged, from_twin, from_across, sems, index):
        self.place = place
        self.staged = staged
        self.from_twin = from_twin
        self.from_across = from_across
        self.sems = sems
        self.index = index

    def twin(self, half):
        return self.place.copy(
            self.staged.at[half],
            self.from_twin.at[half],
            self.sems,
            self.index + half,
            tensor=self.place.twin,
        )

    def crossing(self):
        return self.place.copy(
            self.staged.at[2],
            self.from_across,
            self.sems,
            self.index + 2,
            tensor=self.place.across,
        )

    def give(self, step, values):
        if step == 0 or step == 2:
            half = step // 2
            self.staged[half] = values.astype(BF16)
            self.twin(half).start()
        elif step == 1:
            self.twin(0).wait_recv()
            self.staged[2] = (values + self.from_twin[0].astype(F32)).astype(BF16)
            self.crossing().start()

    def result(self, values):
        self.twin(1).wait_recv()
        self.crossing().wait_recv()
        return values + self.from_twin[1].astype(F32) + self.from_across[...].astype(F32)

    def drain(self):
        self.twin(0).wait_send()
        self.twin(1).wait_send()
        self.crossing().wait_send()


def fill_mixer(mixer):
    row = lax.broadcasted_iota(jnp.int32, mixer.shape, 0) // DH
    column = lax.broadcasted_iota(jnp.int32, mixer.shape, 1) // DH
    mixer[...] = jnp.where(row == column, 1.0 / DH, 0.0).astype(BF16)


class Weights:
    def __init__(self, place, shard, full, outer_sems, inner_sems, piece):
        self.place = place
        self.shard = shard
        self.full = full
        self.outer_sems = outer_sems
        self.inner_sems = inner_sems
        self.piece = piece
        self.rows = shard.shape[0]

    def at(self, index):
        return self.full.at[pl.ds(pl.multiple_of(index * self.rows, self.rows), self.rows), :]

    def outer_copy(self, shift):
        place = self.place
        return place.copy(
            self.shard,
            self.at(place.dp),
            self.outer_sems,
            (self.piece, shift),
            dp=place.ahead(shift),
        )

    def inner_copy(self, shift):
        place = self.place
        rows = self.at(place.behind(shift))
        return place.copy(rows, rows, self.inner_sems, (self.piece, shift), dp=place.other)

    def own_copy(self):
        place = self.place
        return place.copy(
            self.shard, self.at(place.dp), self.inner_sems, (self.piece, 0), dp=place.other
        )

    def send_outer(self):
        @pl.loop(1, self.place.outer_size)
        def _(shift):
            self.outer_copy(shift).start()

    def send_inner(self):
        self.own_copy().start()

    def relay(self, first, last):
        @pl.loop(first, last)
        def _(shift):
            self.outer_copy(shift).wait_recv()
            self.inner_copy(shift).start()

    def finish(self):
        @pl.loop(0, self.place.outer_size)
        def _(shift):
            self.inner_copy(shift).wait_recv()

    def drain(self):
        self.own_copy().wait_send()

        @pl.loop(1, self.place.outer_size)
        def _(shift):
            self.outer_copy(shift).wait_send()
            self.inner_copy(shift).wait_send()


def rotation_angles(length):
    frequency = ROPE_BASE ** (-2.0 * (np.arange(128) % (DH // 2)) / DH)
    steps = np.arange(8) * TILE if length <= 8 * TILE else np.arange(0, length, TILE)
    positions = np.concatenate([np.arange(TILE), steps])
    turns = positions[:, None] * frequency[None, :]
    return jnp.asarray(np.stack([np.cos(turns), np.sin(turns)]).astype(np.float32))


def forward_kernel(
    dp_size,
    turned,
    tokens,
    cotangent,
    segments,
    w_query,
    w_key,
    w_value,
    w_out,
    gate_shard,
    up_shard,
    w_down,
    attn_gain,
    ffn_gain,
    query_gain,
    key_gain,
    angles,
    out_qkv_full,
    out_back_full,
    out_gate_full,
    out_up_full,
    out_down_full,
    out_normed,
    out_ffn,
    out_cot,
    out_gate_slope,
    out_up_slope,
    out_hidden,
    out_grad_down,
    out_query,
    out_key,
    out_value,
    out_attended,
    out_proj,
    out_middle,
    out_tables,
    qkv_shard,
    back_shard,
    down_shard,
    tables,
    query_marks,
    key_marks,
    mixer,
    normed,
    ffn_all,
    cot_all,
    qkv_full,
    back_full,
    gate_full,
    up_full,
    slopes,
    hidden,
    grad_down,
    query,
    key,
    value,
    attended,
    proj,
    middle,
    staged,
    from_twin,
    from_across,
    outer_send,
    outer_recv,
    inner_send,
    inner_recv,
    group_send,
    group_recv,
    local_sems,
    slope_sems,
):
    place = Place(dp_size)
    micro_count = tokens.shape[0]
    block_count = normed.shape[1] // TILE
    outer_size = place.outer_size
    group_sems = (group_send, group_recv)
    outer_sems = (outer_send, outer_recv)
    inner_sems = (inner_send, inner_recv)
    own = tile(place.tensor)
    first_cut = 1 + (outer_size - 1) // 3
    second_cut = 1 + 2 * (outer_size - 1) // 3
    qkv_w = Weights(place, qkv_shard, qkv_full, outer_sems, inner_sems, 0)
    back_w = Weights(place, back_shard, back_full, outer_sems, inner_sems, 1)
    gate_w = Weights(place, gate_shard, gate_full, outer_sems, inner_sems, 2)
    up_w = Weights(place, up_shard, up_full, outer_sems, inner_sems, 3)
    down_w = Weights(place, down_shard, out_down_full, outer_sems, inner_sems, 4)
    normed_g = [Gather(place, normed, m, group_sems, 3 * m) for m in range(micro_count)]
    cot_g = [
        Gather(place, cot_all, m, group_sems, 6 + 3 * m, cotangent.at[m])
        for m in range(micro_count)
    ]
    ffn_g = [Gather(place, ffn_all, m, group_sems, 12 + 3 * m) for m in range(micro_count)]

    def branch_s(m):
        return Scatter(
            place, staged.at[m], from_twin.at[m], from_across.at[m], group_sems, 18 + 3 * m
        )

    saves = []

    def save(src, dst):
        copy = pltpu.make_async_copy(src, dst, local_sems.at[len(saves)])
        copy.start()
        saves.append(copy)
        return copy

    lane = lax.broadcasted_iota(jnp.int32, (TILE, 128), 1)
    front = lane < 64
    place_in = rem(lane, 64)

    value_end = w_query.shape[1] + w_key.shape[1]
    qkv_shard[:, : w_query.shape[1]] = w_query[...]
    qkv_shard[:, w_query.shape[1] : value_end] = w_key[...]
    qkv_shard[:, value_end:] = w_value[...]
    for m in range(micro_count):
        normed[m, own] = norm_rows(tokens[m].astype(F32), attn_gain[...]).astype(BF16)
    if turned:
        back_shard[...] = w_out[...]
        down_shard[...] = w_down[...]
    else:
        back_shard[...] = w_out[...].T
        down_shard[...] = w_down[...].T
    place.greet(False)
    qkv_w.send_outer()
    qkv_w.send_inner()
    normed_g[0].start()
    normed_g[1].start()
    cot_g[0].start()

    def prepare():
        fill_mixer(mixer)
        sign = jnp.where(place_in < 32, -1.0, 1.0)
        for kind, (gain_ref, scale) in enumerate(((query_gain, DH**-0.5 / LN2), (key_gain, 1.0))):
            gain = jnp.broadcast_to(
                jnp.concatenate([gain_ref[...], gain_ref[...]], axis=1) * scale, (TILE, 128)
            )
            crossed = swap_halves(gain) * sign
            for block in range(block_count):
                rows = slice(block * TILE, (block + 1) * TILE)
                cos_step = angles[0, TILE + block : TILE + block + 1]
                sin_step = angles[1, TILE + block : TILE + block + 1]
                cosine = angles[0, 0:TILE] * cos_step - angles[1, 0:TILE] * sin_step
                sine = angles[1, 0:TILE] * cos_step + angles[0, 0:TILE] * sin_step
                tables[2 * kind, rows] = cosine * gain
                tables[2 * kind + 1, rows] = sine * crossed
        row = lax.broadcasted_iota(jnp.int32, (16, 128), 0)
        mark_lane = lax.broadcasted_iota(jnp.int32, (16, 128), 1)
        spread = jnp.where(mark_lane == row + 8, 1.0, 0.0).astype(BF16)
        used = (lane >= 8) & (lane < 11)
        for m in range(micro_count):
            for block in range(block_count):
                rows = slice(block * TILE, (block + 1) * TILE)
                ids = jnp.broadcast_to(segments[m : m + 1, rows], (16, TILE))
                match = lax.broadcasted_iota(jnp.int32, (16, TILE), 0) == ids
                marks = tn(jnp.where(match, 1.0, 0.0).astype(BF16), spread)
                query_marks[m, rows] = marks.astype(BF16)
                apart = jnp.where(used, APART * (1.0 - marks), 0.0)
                for head in range(2):
                    chosen = (lane >= 64 * head) & (lane < 64 * head + 3)
                    key_marks[head, m, rows] = jnp.where(chosen, 1.0, apart).astype(BF16)
        qkv_w.at(place.dp)[...] = qkv_shard[...]
        back_w.at(place.dp)[...] = back_shard[...]
        gate_w.at(place.dp)[...] = gate_shard[...]
        up_w.at(place.dp)[...] = up_shard[...]
        for m in range(micro_count):
            cot_all[m, own] = cotangent[m]

    prepare()
    save(down_shard, down_w.at(place.dp))
    save(tables, out_tables)
    qkv_w.relay(1, second_cut)
    back_w.send_outer()
    qkv_w.relay(second_cut, outer_size)
    back_w.send_inner()
    gate_w.send_outer()
    gate_w.send_inner()
    up_w.send_outer()
    down_w.send_outer()

    later = lax.broadcasted_iota(jnp.int32, (TILE, TILE), 1) > lax.broadcasted_iota(
        jnp.int32, (TILE, TILE), 0
    )
    causal = jnp.where(later, APART, 0.0)

    def project(m):
        @pl.loop(0, block_count)
        def _(block):
            rows = tile(block)
            product = nn(normed[m, rows], qkv_full[...])
            proj[m, rows] = product[:, :384]
            heads = product[:, :256]
            inverse = lax.rsqrt(head_mean(heads * heads, mixer[...]) + NORM_EPS)
            for group in range(2):
                lanes = slice(128 * group, 128 * group + 128)
                part = heads[:, lanes]
                turned = part * tables[0, rows] + swap_halves(part) * tables[1, rows]
                query[m, group, rows, 0:128] = (turned * inverse[:, lanes]).astype(BF16)
                query[m, group, rows, 128:256] = query_marks[m, rows]
            part = product[:, 256:384]
            inverse = lax.rsqrt(head_mean(part * part, mixer[0:128, 0:128]) + NORM_EPS)
            turned = (part * tables[2, rows] + swap_halves(part) * tables[3, rows]) * inverse
            moved = pltpu.roll(turned, 64, 1)
            val = product[:, 384:512]
            val_moved = pltpu.roll(val, 64, 1)
            for group in range(2):
                first, second = (turned, moved) if group == 0 else (moved, turned)
                key[m, group, 0, rows, 0:128] = jnp.where(front, first, 0.0).astype(BF16)
                key[m, group, 1, rows, 0:128] = jnp.where(front, 0.0, second).astype(BF16)
                first, second = (val, val_moved) if group == 0 else (val_moved, val)
                value[m, group, 0, rows, 0:128] = jnp.where(front, first, 0.0).astype(BF16)
                value[m, group, 1, rows, 0:128] = jnp.where(front, 0.0, second).astype(BF16)
                for head in range(2):
                    key[m, group, head, rows, 128:256] = key_marks[head, m, rows]
                value[m, group, 0, rows, 128:256] = jnp.where(front, 1.0, 0.0).astype(BF16)
                value[m, group, 1, rows, 128:256] = jnp.where(front, 0.0, 1.0).astype(BF16)

    def attend(m):
        @pl.loop(0, 2)
        def _(group):
            for block in range(block_count):
                rows = slice(block * TILE, (block + 1) * TILE)
                query_block = query[m, group, rows]
                total = jnp.zeros((TILE, 256), F32)
                for head in range(2):
                    if block > 0:
                        before = slice(0, block * TILE)
                        scores = nt(query_block, key[m, group, head, before])
                        weights = jnp.exp2(scores).astype(BF16)
                        total = total + nn(weights, value[m, group, head, before])
                    scores = nt(query_block, key[m, group, head, rows]) + causal
                    weights = jnp.exp2(scores).astype(BF16)
                    total = total + nn(weights, value[m, group, head, rows])
                sums = total[:, 128:256]
                attended[m, group, rows] = (total[:, 0:128] / sums).astype(BF16)
                shift = -jnp.log2(sums)
                high = shift.astype(BF16)
                middle_part = (shift - high.astype(F32)).astype(BF16)
                last = (shift - high.astype(F32) - middle_part.astype(F32)).astype(BF16)
                marks = jnp.where(
                    place_in == 0,
                    high.astype(F32),
                    jnp.where(
                        place_in == 1,
                        middle_part.astype(F32),
                        jnp.where(
                            place_in == 2,
                            last.astype(F32),
                            query_block[:, 128:256].astype(F32),
                        ),
                    ),
                )
                query[m, group, rows, 128:256] = marks.astype(BF16)

    def branch_block(m, step):
        rows = tile(place.block(step))
        heads = jnp.concatenate([attended[m, 0, rows], attended[m, 1, rows]], axis=1)
        return nt(heads, back_full[...])

    def branch(m):
        for step in range(3):
            branch_s(m).give(step, branch_block(m, step))

    def enter_ffn(m):
        total = branch_s(m).result(branch_block(m, 3))
        middle[m] = tokens[m].astype(F32) + total
        save(middle.at[m], out_middle.at[m])
        ffn_all[m, own] = norm_rows(middle[m], ffn_gain[...]).astype(BF16)
        ffn_g[m].start()

    @pl.loop(0, micro_count)
    def _(m):
        @pl.when(m == 0)
        def _():
            normed_g[0].relay()
            normed_g[0].finish()
            qkv_w.finish()

        @pl.when(m == 1)
        def _():
            normed_g[1].finish()

        project(m)

        @pl.when(m == 0)
        def _():
            back_w.relay(1, outer_size)
            up_w.send_inner()

        @pl.when(m == 1)
        def _():
            gate_w.relay(1, first_cut)

        attend(m)

        @pl.when(m == 0)
        def _():
            normed_g[1].relay()
            back_w.finish()

        @pl.when(m == 1)
        def _():
            down_w.send_inner()

        branch(m)

    save(qkv_full, out_qkv_full)
    save(back_full, out_back_full)
    for m in range(micro_count):
        save(query.at[m], out_query.at[m])
        save(key.at[m], out_key.at[m])
        save(value.at[m], out_value.at[m])
        save(attended.at[m], out_attended.at[m])
        save(proj.at[m], out_proj.at[m])
        save(normed.at[m], out_normed.at[m])
    gate_w.relay(first_cut, second_cut)
    cot_g[0].relay()
    gate_w.relay(second_cut, outer_size)
    enter_ffn(0)
    up_w.relay(1, first_cut)
    enter_ffn(1)
    cot_g[1].start()
    up_w.relay(first_cut, second_cut)
    cot_g[0].finish()
    save(cot_all.at[0], out_cot.at[0])
    gate_w.finish()
    save(gate_full, out_gate_full)
    up_w.relay(second_cut, outer_size)
    ffn_g[0].relay()
    ffn_g[0].finish()
    save(ffn_all.at[0], out_ffn.at[0])
    up_w.finish()
    save(up_full, out_up_full)

    def slope_copies(index):
        m = index // block_count
        rows = tile(rem(index, block_count))
        slot = rem(index, 2)
        return [
            pltpu.make_async_copy(
                slopes.at[slot, kind], out.at[m, rows], slope_sems.at[slot, kind]
            )
            for kind, out in enumerate((out_gate_slope, out_up_slope))
        ]

    tile_count = micro_count * block_count

    @pl.loop(0, tile_count)
    def _(index):
        m = index // block_count
        rows = tile(rem(index, block_count))
        slot = rem(index, 2)

        @pl.when(index >= 2)
        def _():
            for copy in slope_copies(index - 2):
                copy.wait()

        @pl.when(index == 2)
        def _():
            down_w.relay(1, first_cut)

        @pl.when(index == block_count)
        def _():
            ffn_g[1].relay()
            ffn_g[1].finish()

        @pl.when(index == block_count + 2)
        def _():
            down_w.relay(first_cut, second_cut)

        gate = nn(ffn_all[m, rows], gate_full[...])
        up = nn(ffn_all[m, rows], up_full[...])
        sig = 1.0 / (1.0 + jnp.exp(-gate))
        act = gate * sig
        hidden[m, rows] = (act * up).astype(BF16)
        slopes[slot, 0] = (up * (sig + act * (1.0 - sig))).astype(BF16)
        slopes[slot, 1] = act.astype(BF16)
        for copy in slope_copies(index):
            copy.start()

    save(ffn_all.at[1], out_ffn.at[1])
    save(hidden, out_hidden)
    for index in (tile_count - 2, tile_count - 1):
        for copy in slope_copies(index):
            copy.wait()
    cot_g[1].relay()
    down_w.relay(second_cut, outer_size)
    cot_g[1].finish()
    save(cot_all.at[1], out_cot.at[1])

    @pl.loop(0, block_count)
    def _(block):
        columns = tile(block)
        grad_down[columns] = (
            tn(cot_all[0, :, columns], hidden[0]) + tn(cot_all[1, :, columns], hidden[1])
        ).astype(BF16)

    save(grad_down, out_grad_down)
    down_w.finish()
    for piece in (qkv_w, back_w, gate_w, up_w, down_w):
        piece.drain()
    for m in range(micro_count):
        normed_g[m].drain()
        cot_g[m].drain()
        ffn_g[m].drain()
        branch_s(m).drain()
    for copy in saves:
        copy.wait()


def forward(dp_size, tokens, cotangent, segments, weights, gains):
    w_query, w_key, w_value, w_out, w_gate, w_up, w_down = weights
    micro, rows, width = tokens.shape
    length = segments.shape[1]
    share, hidden_width = w_gate.shape
    qkv_width = w_query.shape[1] + w_key.shape[1] + w_value.shape[1]
    back_width = w_out.shape[0]
    turned = share % 128 != 0
    if turned:
        w_out, w_down = w_out.T, w_down.T
    outer_size = dp_size // 2
    whole = pl.BlockSpec(memory_space=pltpu.VMEM)
    anywhere = pl.BlockSpec(memory_space=pl.ANY)
    shape = jax.ShapeDtypeStruct
    out_shape = [
        shape((width, qkv_width), BF16),
        shape((width, back_width), BF16),
        shape((width, hidden_width), BF16),
        shape((width, hidden_width), BF16),
        shape((width, hidden_width), BF16),
        shape((micro, length, width), BF16),
        shape((micro, length, width), BF16),
        shape((micro, length, width), BF16),
        shape((micro, length, hidden_width), BF16),
        shape((micro, length, hidden_width), BF16),
        shape((micro, length, hidden_width), BF16),
        shape((width, hidden_width), BF16),
        shape((micro, 2, length, 256), BF16),
        shape((micro, 2, 2, length, 256), BF16),
        shape((micro, 2, 2, length, 256), BF16),
        shape((micro, 2, length, 128), BF16),
        shape((micro, length, 384), F32),
        shape((micro, rows, width), F32),
        shape((4, length, 128), F32),
    ]
    scratch = [
        pltpu.VMEM((share, qkv_width), BF16),
        pltpu.VMEM((share, back_width), BF16),
        pltpu.VMEM((share, hidden_width), BF16),
        pltpu.VMEM((4, length, 128), F32),
        pltpu.VMEM((micro, length, 128), BF16),
        pltpu.VMEM((2, micro, length, 128), BF16),
        pltpu.VMEM((256, 256), BF16),
        pltpu.VMEM((micro, length, width), BF16),
        pltpu.VMEM((micro, length, width), BF16),
        pltpu.VMEM((micro, length, width), BF16),
        pltpu.VMEM((width, qkv_width), BF16),
        pltpu.VMEM((width, back_width), BF16),
        pltpu.VMEM((width, hidden_width), BF16),
        pltpu.VMEM((width, hidden_width), BF16),
        pltpu.VMEM((2, 2, TILE, hidden_width), BF16),
        pltpu.VMEM((micro, length, hidden_width), BF16),
        pltpu.VMEM((width, hidden_width), BF16),
        pltpu.VMEM((micro, 2, length, 256), BF16),
        pltpu.VMEM((micro, 2, 2, length, 256), BF16),
        pltpu.VMEM((micro, 2, 2, length, 256), BF16),
        pltpu.VMEM((micro, 2, length, 128), BF16),
        pltpu.VMEM((micro, length, 384), F32),
        pltpu.VMEM((micro, rows, width), F32),
        pltpu.VMEM((micro, 3, rows, width), BF16),
        pltpu.VMEM((micro, 2, rows, width), BF16),
        pltpu.VMEM((micro, rows, width), BF16),
        pltpu.SemaphoreType.DMA((5, outer_size)),
        pltpu.SemaphoreType.DMA((5, outer_size)),
        pltpu.SemaphoreType.DMA((5, outer_size)),
        pltpu.SemaphoreType.DMA((5, outer_size)),
        pltpu.SemaphoreType.DMA((24,)),
        pltpu.SemaphoreType.DMA((24,)),
        pltpu.SemaphoreType.DMA((32,)),
        pltpu.SemaphoreType.DMA((2, 2)),
    ]
    operands = (
        tokens,
        cotangent,
        segments,
        w_query,
        w_key,
        w_value,
        w_out,
        w_gate,
        w_up,
        w_down,
        *gains,
        rotation_angles(length),
    )
    return pl.pallas_call(
        functools.partial(forward_kernel, dp_size, turned),
        out_shape=out_shape,
        in_specs=[whole] * len(operands),
        out_specs=[anywhere] * len(out_shape),
        scratch_shapes=scratch,
        compiler_params=pltpu.CompilerParams(
            collective_id=0, has_side_effects=True, vmem_limit_bytes=VMEM_LIMIT
        ),
        name="forward_pass",
    )(*operands)


class Shares:
    def __init__(self, place, partial, kept, from_inner, from_outer, outer_sems, inner_sems, piece):
        self.place = place
        self.partial = partial
        self.kept = kept
        self.from_inner = from_inner
        self.from_outer = from_outer
        self.outer_sems = outer_sems
        self.inner_sems = inner_sems
        self.piece = piece
        self.rows = from_inner.shape[1]

    def at(self, index):
        return self.partial.at[pl.ds(pl.multiple_of(index * self.rows, self.rows), self.rows), :]

    def mine(self, shift):
        if self.kept is not None:
            return self.kept.at[shift]
        return self.at(self.place.ahead(shift))

    def inner_copy(self, shift):
        place = self.place
        return place.copy(
            self.at(place.ahead(shift, 1 - place.inner)),
            self.from_inner.at[shift],
            self.inner_sems,
            (self.piece, shift),
            dp=place.other,
        )

    def outer_copy(self, shift):
        place = self.place
        return place.copy(
            self.mine(shift),
            self.from_outer.at[shift - 1],
            self.outer_sems,
            (self.piece, shift),
            dp=place.ahead(shift),
        )

    def give(self):
        @pl.loop(1, self.place.outer_size)
        def _(shift):
            self.inner_copy(shift).start()

        self.inner_copy(0).start()

    def turn(self, first, last):
        @pl.loop(first, last)
        def _(shift):
            self.inner_copy(shift).wait_recv()
            mine = self.mine(shift)
            mine[...] = (mine[...].astype(F32) + self.from_inner[shift].astype(F32)).astype(BF16)
            self.outer_copy(shift).start()

    def keep(self, total):
        self.inner_copy(0).wait_recv()
        total[...] = self.mine(0)[...].astype(F32) + self.from_inner[0].astype(F32)

    def finish(self, total):
        @pl.loop(1, self.place.outer_size)
        def _(shift):
            self.outer_copy(shift).wait_recv()
            total[...] += self.from_outer[shift - 1].astype(F32)

    def drain(self):
        self.inner_copy(0).wait_send()

        @pl.loop(1, self.place.outer_size)
        def _(shift):
            self.inner_copy(shift).wait_send()
            self.outer_copy(shift).wait_send()


def backward_kernel(
    dp_size,
    cotangent,
    attn_gain,
    ffn_gain,
    tokens,
    qkv_full,
    back_full,
    gate_full,
    up_full,
    down_full,
    normed,
    ffn_all,
    cot_all,
    gate_slope,
    up_slope,
    hidden,
    grad_down,
    query,
    key,
    value,
    attended,
    proj,
    middle_in,
    tables,
    out_mixed,
    out_tokens,
    gain_sums,
    out_qkv,
    out_back,
    out_gate,
    out_up,
    out_down,
    mixed,
    mid_all,
    mixer,
    ffn_w,
    down_w,
    qkv_w,
    att,
    qry,
    ky,
    val,
    prj,
    down_kept,
    qkv_inner,
    back_inner,
    ffn_inner,
    down_inner,
    qkv_outer,
    back_outer,
    ffn_outer,
    down_outer,
    staged,
    part_twin,
    part_across,
    out_twin,
    out_across,
    middle,
    gain_parts,
    gain_packed,
    gain_group,
    gain_dp,
    outer_send,
    outer_recv,
    inner_send,
    inner_recv,
    group_send,
    group_recv,
    gain_send,
    gain_recv,
    local_sems,
    tile_sems,
):
    place = Place(dp_size)
    micro_count = mixed.shape[0]
    length = mid_all.shape[1]
    width = mid_all.shape[2]
    hidden_width = down_w.shape[1]
    block_count = length // TILE
    tile_count = micro_count * block_count
    outer_size = place.outer_size
    group_sems = (group_send, group_recv)
    outer_sems = (outer_send, outer_recv)
    inner_sems = (inner_send, inner_recv)
    own = tile(place.tensor)
    first_cut = 1 + (outer_size - 1) // 3
    second_cut = 1 + 2 * (outer_size - 1) // 3
    outers = outer_size // 4
    own_outer_block = place.outer // outers
    counter = []

    def load(src, dst):
        copy = pltpu.make_async_copy(src, dst, local_sems.at[len(counter) + (8 if len(counter) >= 8 else 0)])
        counter.append(copy)
        copy.start()
        return copy

    down_s = Shares(place, grad_down, down_kept, down_inner, down_outer, outer_sems, inner_sems, 4)

    def ffn_shares(kind):
        return Shares(
            place,
            ffn_w.at[kind],
            None,
            ffn_inner.at[kind],
            ffn_outer.at[kind],
            outer_sems,
            inner_sems,
            2 + kind,
        )

    gate_s, up_s = ffn_shares(0), ffn_shares(1)
    mid_g = [Gather(place, mid_all, m, group_sems, 3 * m) for m in range(micro_count)]

    def turn_block(step):
        return rem(step + 1 + own_outer_block, 4)

    def give_block(share, block):
        @pl.loop(0, outers)
        def _(index):
            shift = rem(block * outers + index - place.outer + outer_size, outer_size)
            share.inner_copy(shift).start()

    def twin_copy(kind, m, half):
        from_twin = (part_twin, out_twin, part_twin)[kind]
        return place.copy(
            staged.at[m, half],
            from_twin.at[m, half],
            group_sems,
            6 + 6 * kind + 3 * m + half,
            tensor=place.twin,
        )

    def across_copy(kind, m):
        from_across = (part_across, out_across, part_across)[kind]
        return place.copy(
            staged.at[m, 2],
            from_across.at[m],
            group_sems,
            6 + 6 * kind + 3 * m + 2,
            tensor=place.across,
        )

    def block_of(step):
        side = jnp.where(step < 2, 1 - place.side, place.side)
        core = jnp.where(rem(step, 2) == 0, 1 - place.core, place.core)
        return side * 2 + core

    def hand_out(kind, m, step, values):
        from_twin = (part_twin, out_twin, part_twin)[kind]
        half = step // 2

        @pl.when(rem(step, 2) == 0)
        def _():
            staged[m, half] = values.astype(BF16)
            twin_copy(kind, m, half).start()

        @pl.when(step == 1)
        def _():
            twin_copy(kind, m, 0).wait_recv()
            staged[m, 2] = (values + from_twin[m, 0].astype(F32)).astype(BF16)
            across_copy(kind, m).start()

        @pl.when(step == 3)
        def _():
            staged[m, 3] = values.astype(BF16)

    def collect(kind, m):
        from_twin = (part_twin, out_twin, part_twin)[kind]
        from_across = (part_across, out_across, part_across)[kind]
        twin_copy(kind, m, 1).wait_recv()
        across_copy(kind, m).wait_recv()
        return staged[m, 3].astype(F32) + from_twin[m, 1].astype(F32) + from_across[m].astype(F32)

    def drain(kind, m):
        twin_copy(kind, m, 0).wait_send()
        twin_copy(kind, m, 1).wait_send()
        across_copy(kind, m).wait_send()

    def leave_ffn(m):
        upstream = collect(0, m)
        back, term = norm_rows_back(middle[m], ffn_gain[...], upstream)
        mid_all[m, own] = (mixed[m].astype(F32) + back).astype(BF16)
        mid_g[m].start()
        gain_parts[1:2, :] += term

    def leave_out(m):
        mixed[m] = (middle[m] + collect(1, m)).astype(BF16)

    def attn_copies():
        pairs = (
            (back_full, qkv_w.at[:, 512:768]),
            (attended, att),
            (value.at[0], val),
            (key.at[0], ky),
            (query.at[0], qry),
            (proj.at[0], prj),
            (qkv_full, qkv_w.at[:, 0:512]),
        )
        return [
            pltpu.make_async_copy(src, dst, local_sems.at[30 + index])
            for index, (src, dst) in enumerate(pairs)
        ]

    def ffn_phase(grads, rows_buf, hidden_buf, ffn_cols):
        def rows_copy(index):
            m = index // block_count
            rows = tile(block_of(rem(index, block_count)))
            slot = rem(index, 2)
            return pltpu.make_async_copy(cot_all.at[m, rows], rows_buf.at[slot], tile_sems.at[0, slot])

        def hidden_copy(index):
            m = index // block_count
            rows = tile(block_of(rem(index, block_count)))
            slot = rem(index, 2)
            return pltpu.make_async_copy(hidden.at[m, rows], hidden_buf.at[slot], tile_sems.at[1, slot])

        def cols_copy(index):
            slot = rem(index, 2)
            return pltpu.make_async_copy(
                ffn_all.at[:, :, tile(turn_block(rem(index, block_count)))],
                ffn_cols.at[slot],
                tile_sems.at[2, slot],
            )

        loads = [load(down_full, down_w)]
        rows_copy(0).start()
        loads += [load(gate_slope.at[0], grads.at[0, 0]), load(up_slope.at[0], grads.at[1, 0])]
        loads += [load(gate_full, ffn_w.at[0]), load(up_full, ffn_w.at[1]), load(middle_in, middle)]
        loads.append(load(cotangent, mixed))

        def second_copies():
            return [
                pltpu.make_async_copy(slope.at[1], grads.at[kind, 1], local_sems.at[38 + kind])
                for kind, slope in enumerate((gate_slope, up_slope))
            ]

        def kept_copy(shift):
            return pltpu.make_async_copy(
                down_s.at(place.ahead(shift)), down_kept.at[shift], local_sems.at[40 + shift]
            )

        for copy in second_copies():
            copy.start()

        @pl.loop(0, outer_size)
        def _(shift):
            kept_copy(shift).start()

        fill_mixer(mixer)
        gain_parts[...] = jnp.zeros_like(gain_parts)
        gain_packed[...] = jnp.zeros_like(gain_packed)
        place.greet(True)
        down_s.give()
        for copy in loads:
            copy.wait()

        @pl.loop(0, tile_count)
        def _(index):
            m = index // block_count
            step = rem(index, block_count)
            rows = tile(block_of(step))
            slot = rem(index, 2)

            @pl.when(index + 1 < tile_count)
            def _():
                rows_copy(index + 1).start()

            @pl.when(index == 2)
            def _():
                @pl.loop(0, outer_size)
                def _(shift):
                    kept_copy(shift).wait()

                down_s.turn(1, first_cut)

            @pl.when(index == block_count)
            def _():
                for copy in second_copies():
                    copy.wait()

            @pl.when(index == block_count + 1)
            def _():
                down_s.turn(first_cut, second_cut)

            @pl.when(index == block_count + 3)
            def _():
                down_s.turn(second_cut, outer_size)
                leave_ffn(0)

            rows_copy(index).wait()
            hidden_grad = nn(rows_buf[slot], down_w[...])
            gate_low = (hidden_grad * grads[0, m, rows].astype(F32)).astype(BF16)
            up_low = (hidden_grad * grads[1, m, rows].astype(F32)).astype(BF16)
            grads[0, m, rows] = gate_low
            grads[1, m, rows] = up_low
            hand_out(0, m, step, nt(gate_low, ffn_w[0]) + nt(up_low, ffn_w[1]))

        for copy in attn_copies():
            copy.start()
        cols_copy(0).start()

        @pl.loop(0, 2 * block_count)
        def _(index):
            kind = index // block_count
            block = turn_block(rem(index, block_count))
            slot = rem(index, 2)
            cols_copy(index).wait()

            @pl.when(index + 1 < 2 * block_count)
            def _():
                cols_copy(index + 1).start()

            ffn_w[kind, tile(block)] = (
                tn(ffn_cols[slot, 0], grads[kind, 0]) + tn(ffn_cols[slot, 1], grads[kind, 1])
            ).astype(BF16)
            give_block(ffn_shares(kind), block)

            @pl.when(index == block_count + 2)
            def _():
                leave_ffn(1)

        hidden_copy(0).start()

        @pl.loop(0, tile_count)
        def _(index):
            m = index // block_count
            step = rem(index, block_count)
            slot = rem(index, 2)

            @pl.when(index + 1 < tile_count)
            def _():
                hidden_copy(index + 1).start()

            hidden_copy(index).wait()

            @pl.when(step == 0)
            def _():
                drain(0, m)

            hand_out(1, m, step, nt(hidden_buf[slot], down_w[...]))

    pl.run_scoped(
        ffn_phase,
        pltpu.VMEM((2, micro_count, length, hidden_width), BF16),
        pltpu.VMEM((2, TILE, width), BF16),
        pltpu.VMEM((2, TILE, hidden_width), BF16),
        pltpu.VMEM((2, micro_count, length, TILE), BF16),
    )

    def attn_phase(
        toks,
        tabs,
        grad_att,
        grad_q,
        grad_k,
        grad_v,
        grad_qkv,
        qkv_total,
        back_total,
        gate_total,
        up_total,
        down_total,
    ):
        qkv_part = down_w.at[:, 0:512]
        back_part = down_w.at[:, 512:768]
        qkv_s = Shares(place, qkv_part, None, qkv_inner, qkv_outer, outer_sems, inner_sems, 0)
        back_s = Shares(place, back_part, None, back_inner, back_outer, outer_sems, inner_sems, 1)
        lane = lax.broadcasted_iota(jnp.int32, (TILE, 128), 1)
        front = lane < 64
        place_in = rem(lane, 64)
        later = lax.broadcasted_iota(jnp.int32, (TILE, TILE), 0) > lax.broadcasted_iota(
            jnp.int32, (TILE, TILE), 1
        )
        causal = jnp.where(later, APART, 0.0)
        small = mixer[0:128, 0:128]
        table_load = load(tables, tabs)
        token_load = load(tokens, toks)

        def score_ready(m):
            @pl.loop(0, block_count)
            def _(block):
                rows = tile(block)
                low = nn(mid_all[m, rows], qkv_w[:, 512:768]).astype(BF16)
                for group in range(2):
                    part = low[:, 128 * group : 128 * group + 128]
                    both = part.astype(F32) * att[m, group, rows].astype(F32)
                    shift = head_mean(both, small) * -64.0
                    high = shift.astype(BF16)
                    rest = shift - high.astype(F32)
                    mid = rest.astype(BF16)
                    last = (rest - mid.astype(F32)).astype(BF16)
                    marks = jnp.where(
                        place_in == 0,
                        high.astype(F32),
                        jnp.where(
                            place_in == 1,
                            mid.astype(F32),
                            jnp.where(place_in == 2, last.astype(F32), 0.0),
                        ),
                    )
                    grad_att[group, rows, 0:128] = part
                    grad_att[group, rows, 128:256] = marks.astype(BF16)

        def attend_back(m, between):
            @pl.loop(0, 2)
            def _(group):
                for block in range(block_count):
                    rows = slice(block * TILE, (block + 1) * TILE)
                    spans = [(rows, True)]
                    if block + 1 < block_count:
                        spans.append((slice((block + 1) * TILE, length), False))
                    sums_k = []
                    sums_v = []
                    for head in range(2):
                        key_block = ky[group, head, rows]
                        value_block = val[group, head, rows]
                        sum_k = None
                        sum_v = None
                        for span, masked in spans:
                            query_span = qry[group, span]
                            grad_span = grad_att[group, span]
                            scores = nt(key_block, query_span)
                            if masked:
                                scores = scores + causal
                            probs = jnp.exp2(scores)
                            score_grad = (probs * nt(value_block, grad_span)).astype(BF16)
                            probs_low = probs.astype(BF16)
                            part_v = nn(probs_low, grad_span[:, 0:128])
                            part_k = nn(score_grad, query_span[:, 0:128])
                            sum_v = part_v if sum_v is None else sum_v + part_v
                            sum_k = part_k if sum_k is None else sum_k + part_k
                            part_q = tn(score_grad, key_block[:, 0:128])
                            if block == 0 and head == 0:
                                grad_q[group, span] = part_q
                            else:
                                grad_q[group, span] += part_q
                        sums_k.append(sum_k)
                        sums_v.append(sum_v)
                    both_k = jnp.where(front, sums_k[0], sums_k[1])
                    both_v = jnp.where(front, sums_v[0], sums_v[1])
                    grad_k[group, rows] = both_k + pltpu.roll(both_k, 64, 1)
                    grad_v[group, rows] = both_v + pltpu.roll(both_v, 64, 1)

                @pl.when(group == 0)
                def _():
                    between()

        def normalize_back(grads, values, cosine, sine):
            scaled = grads * LN2
            weighted = scaled * cosine + swap_halves(scaled * sine)
            inverse = lax.rsqrt(head_mean(values * values, small) + NORM_EPS)
            unit = values * inverse
            both = weighted * unit
            back = inverse * (weighted - unit * head_mean(both, small))
            return back.astype(BF16), jnp.sum(both, axis=0, keepdims=True)

        def leave_heads(m):
            @pl.loop(0, block_count)
            def _(block):
                rows = tile(block)
                cosine, sine = tabs[0, rows], tabs[1, rows]
                for group in range(2):
                    lanes = slice(128 * group, 128 * group + 128)
                    back, term = normalize_back(grad_q[group, rows], prj[rows, lanes], cosine, sine)
                    grad_qkv[m, rows, lanes] = back
                    gain_parts[2:3, 0:128] += term
                back, term = normalize_back(
                    jnp.where(front, grad_k[0, rows], grad_k[1, rows]),
                    prj[rows, 256:384],
                    tabs[2, rows],
                    tabs[3, rows],
                )
                grad_qkv[m, rows, 256:384] = back
                gain_parts[2:3, 128:256] += term
                grad_qkv[m, rows, 384:512] = jnp.where(
                    front, grad_v[0, rows], grad_v[1, rows]
                ).astype(BF16)

        def enter_norm(m):
            drain(1, m)

            @pl.loop(0, block_count)
            def _(step):
                rows = tile(block_of(step))
                hand_out(2, m, step, nt(grad_qkv[m, rows], qkv_w[:, 0:512]))

        def leave_attn(m):
            upstream = collect(2, m)
            back, term = norm_rows_back(toks[m].astype(F32), attn_gain[...], upstream)
            middle[m] = mid_all[m, own].astype(F32) + back
            gain_parts[0:1, :] += term

        def norm_copy(index):
            slot = rem(index, 2)
            return pltpu.make_async_copy(
                normed.at[:, :, tile(turn_block(index))], val.at[slot], tile_sems.at[3, slot]
            )

        reloads = ((value, val), (key, ky), (query, qry), (proj, prj))

        def reload_copy(index):
            src, dst = reloads[index]
            return pltpu.make_async_copy(src.at[1], dst, local_sems.at[10 + index])

        def mixed_save(m):
            return pltpu.make_async_copy(mixed.at[m], out_mixed.at[m], local_sems.at[14 + m])

        def enter_back():
            @pl.loop(0, block_count)
            def _(step):
                block = turn_block(step)
                columns = tile(block)
                total = jnp.zeros((TILE, 256), F32)
                for m in range(micro_count):
                    heads = jnp.concatenate([att[m, 0], att[m, 1]], axis=1)
                    total = total + tn(mid_all[m, :, columns], heads)
                back_part[columns] = total.astype(BF16)
                give_block(back_s, block)

        table_load.wait()
        token_load.wait()

        @pl.loop(0, micro_count)
        def _(m):
            @pl.when(m == 0)
            def _():
                down_s.keep(down_total)
                gate_s.turn(1, first_cut)
                mid_g[0].relay()
                for copy in attn_copies():
                    copy.wait()
                mid_g[0].finish()

            @pl.when(m == 1)
            def _():
                mid_g[1].finish()
                for index in range(4):
                    reload_copy(index).wait()

            score_ready(m)

            @pl.when(m == 0)
            def _():
                gate_s.turn(first_cut, second_cut)

            @pl.when(m == 1)
            def _():
                enter_back()
                up_s.turn(first_cut, second_cut)

            def between():
                @pl.when(m == 0)
                def _():
                    gate_s.turn(second_cut, outer_size)
                    mid_g[1].relay()

                @pl.when(m == 1)
                def _():
                    up_s.turn(second_cut, outer_size)

            attend_back(m, between)

            @pl.when(m == 0)
            def _():
                for index in range(3):
                    reload_copy(index).start()
                gate_s.keep(gate_total)

            @pl.when(m == 1)
            def _():
                norm_copy(0).start()

            leave_heads(m)

            @pl.when(m == 0)
            def _():
                reload_copy(3).start()
                up_s.turn(1, first_cut)

            @pl.when(m == 1)
            def _():
                up_s.keep(up_total)

            leave_out(m)
            mixed_save(m).start()
            enter_norm(m)

        saves = [mixed_save(m) for m in range(micro_count)]
        down_s.finish(down_total)
        saves.append(load(down_total, out_down))
        gate_s.finish(gate_total)
        saves.append(load(gate_total, out_gate))
        back_s.turn(1, outer_size)

        @pl.loop(0, block_count)
        def _(step):
            block = turn_block(step)
            columns = tile(block)
            slot = rem(step, 2)
            norm_copy(step).wait()

            @pl.when(step + 1 < block_count)
            def _():
                norm_copy(step + 1).start()

            qkv_part[columns] = (
                tn(val[slot, 0], grad_qkv[0]) + tn(val[slot, 1], grad_qkv[1])
            ).astype(BF16)
            give_block(qkv_s, block)

        back_s.keep(back_total)
        leave_attn(0)
        saves.append(load(middle.at[0], out_tokens.at[0]))
        qkv_s.turn(1, outer_size)
        up_s.finish(up_total)
        saves.append(load(up_total, out_up))
        leave_attn(1)
        saves.append(load(middle.at[1], out_tokens.at[1]))

        def group_gain(shift):
            return place.copy(
                gain_packed,
                gain_group.at[shift - 1],
                (gain_send, gain_recv),
                shift - 1,
                tensor=rem(place.tensor + shift, 4),
            )

        pack_gains(gain_packed, gain_parts)
        for shift in range(1, 4):
            group_gain(shift).start()
        qkv_s.keep(qkv_total)
        back_s.finish(back_total)
        saves.append(load(back_total, out_back))
        for shift in range(1, 4):
            group_gain(shift).wait_recv()
        gain_dp[0] = gain_packed[...] + gain_group[0] + gain_group[1] + gain_group[2]

        def dp_gain(shift):
            return place.copy(
                gain_dp.at[0],
                gain_dp.at[shift],
                (gain_send, gain_recv),
                2 + shift,
                dp=rem(place.dp + shift, dp_size),
            )

        @pl.loop(1, dp_size)
        def _(shift):
            dp_gain(shift).start()

        qkv_s.finish(qkv_total)
        saves.append(load(qkv_total, out_qkv))
        gain_sums[...] = gain_dp[0]

        @pl.loop(1, dp_size)
        def _(shift):
            dp_gain(shift).wait_recv()
            gain_sums[...] += gain_dp[shift]

        for shift in range(1, 4):
            group_gain(shift).wait_send()

        @pl.loop(1, dp_size)
        def _(shift):
            dp_gain(shift).wait_send()

        qkv_s.drain()
        back_s.drain()
        for copy in saves:
            copy.wait()

    pl.run_scoped(
        attn_phase,
        pltpu.VMEM(tokens.shape, BF16),
        pltpu.VMEM(tables.shape, F32),
        pltpu.VMEM((2, length, 256), BF16),
        pltpu.VMEM((2, length, 128), F32),
        pltpu.VMEM((2, length, 128), F32),
        pltpu.VMEM((2, length, 128), F32),
        pltpu.VMEM((micro_count, length, 512), BF16),
        *[
            pltpu.VMEM((width // dp_size, w), F32)
            for w in (512, 256, hidden_width, hidden_width, hidden_width)
        ],
    )
    for share in (down_s, gate_s, up_s):
        share.drain()
    for m in range(micro_count):
        mid_g[m].drain()
        drain(2, m)


def backward(dp_size, cotangent, attn_gain, ffn_gain, tokens, saved):
    micro, rows, width = tokens.shape
    length = saved[5].shape[1]
    hidden_width = saved[2].shape[1]
    outer_size = dp_size // 2
    share = width // dp_size
    whole = pl.BlockSpec(memory_space=pltpu.VMEM)
    anywhere = pl.BlockSpec(memory_space=pl.ANY)
    shape = jax.ShapeDtypeStruct
    widths = (512, 256, hidden_width, hidden_width, hidden_width)
    out_shape = [
        shape((micro, rows, width), BF16),
        shape((micro, rows, width), F32),
        shape((8, 384), F32),
    ] + [shape((share, w), F32) for w in widths]
    scratch = (
        [pltpu.VMEM((micro, rows, width), BF16)]
        + [
            pltpu.VMEM((micro, length, width), BF16),
            pltpu.VMEM((256, 256), BF16),
            pltpu.VMEM((2, width, hidden_width), BF16),
            pltpu.VMEM((width, hidden_width), BF16),
            pltpu.VMEM((width, 768), BF16),
            pltpu.VMEM((micro, 2, length, 128), BF16),
            pltpu.VMEM((2, length, 256), BF16),
            pltpu.VMEM((2, 2, length, 256), BF16),
            pltpu.VMEM((2, 2, length, 256), BF16),
            pltpu.VMEM((length, 384), F32),
            pltpu.VMEM((outer_size, share, hidden_width), BF16),
            pltpu.VMEM((outer_size, share, 512), BF16),
            pltpu.VMEM((outer_size, share, 256), BF16),
            pltpu.VMEM((2, outer_size, share, hidden_width), BF16),
            pltpu.VMEM((outer_size, share, hidden_width), BF16),
            pltpu.VMEM((outer_size - 1, share, 512), BF16),
            pltpu.VMEM((outer_size - 1, share, 256), BF16),
            pltpu.VMEM((2, outer_size - 1, share, hidden_width), BF16),
            pltpu.VMEM((outer_size - 1, share, hidden_width), BF16),
            pltpu.VMEM((micro, 4, rows, width), BF16),
            pltpu.VMEM((micro, 2, rows, width), BF16),
            pltpu.VMEM((micro, rows, width), BF16),
            pltpu.VMEM((micro, 2, rows, width), BF16),
            pltpu.VMEM((micro, rows, width), BF16),
            pltpu.VMEM((micro, rows, width), F32),
            pltpu.VMEM((8, width), F32),
            pltpu.VMEM((8, 384), F32),
            pltpu.VMEM((3, 8, 384), F32),
            pltpu.VMEM((dp_size, 8, 384), F32),
        ]
        + [pltpu.SemaphoreType.DMA((5, outer_size))] * 4
        + [pltpu.SemaphoreType.DMA((24,))] * 2
        + [pltpu.SemaphoreType.DMA((dp_size + 2,))] * 2
        + [pltpu.SemaphoreType.DMA((40 + outer_size,)), pltpu.SemaphoreType.DMA((4, 2))]
    )
    return pl.pallas_call(
        functools.partial(backward_kernel, dp_size),
        out_shape=out_shape,
        in_specs=[anywhere, whole, whole] + [anywhere] * (1 + len(saved)),
        out_specs=[anywhere, anywhere, whole] + [anywhere] * 5,
        scratch_shapes=scratch,
        compiler_params=pltpu.CompilerParams(
            collective_id=1, has_side_effects=True, vmem_limit_bytes=VMEM_LIMIT
        ),
        name="backward_pass",
    )(cotangent, attn_gain, ffn_gain, tokens, *saved)


def deliver_kernel(
    turned,
    in_mixed,
    in_tokens,
    gains,
    in_qkv,
    in_back,
    in_gate,
    in_up,
    in_down,
    mixed,
    grad_tokens,
    attn_gain,
    ffn_gain,
    head_gains,
    grad_query,
    grad_key,
    grad_value,
    grad_out,
    grad_gate,
    grad_up,
    grad_down,
    buf_mixed,
    buf_tokens,
    buf_gate,
    buf_up,
    buf_qkv,
    buf_back,
    buf_down,
    sems,
):
    flows = [
        (in_qkv, buf_qkv, None),
        (in_back, buf_back, None),
        (in_down, buf_down, None),
        (in_mixed, buf_mixed, mixed),
        (in_tokens.at[0], buf_tokens.at[0], grad_tokens.at[0]),
        (in_tokens.at[1], buf_tokens.at[1], grad_tokens.at[1]),
        (in_gate, buf_gate, grad_gate),
        (in_up, buf_up, grad_up),
    ]
    arrivals = [
        pltpu.make_async_copy(src, buf, sems.at[0, index]) for index, (src, buf, _) in enumerate(flows)
    ]
    departures = []
    for copy in arrivals:
        copy.start()
    part = 0
    for out in (attn_gain, ffn_gain, head_gains):
        for start in range(0, out.shape[1], 128):
            out[:, start : start + 128] = gains[
                part // 3 : part // 3 + 1, 128 * (part % 3) : 128 * (part % 3) + 128
            ]
            part += 1
    for index, (_, buf, dst) in enumerate(flows):
        arrivals[index].wait()
        if dst is not None:
            copy = pltpu.make_async_copy(buf, dst, sems.at[1, index])
            copy.start()
            departures.append(copy)
        if index == 2:
            grad_query[...] = buf_qkv[:, 0:256]
            grad_key[...] = buf_qkv[:, 256:384]
            grad_value[...] = buf_qkv[:, 384:512]
            grad_out[...] = buf_back[...] if turned else buf_back[...].T
            grad_down[...] = buf_down[...] if turned else buf_down[...].T
    for copy in departures:
        copy.wait()


def deliver(results):
    mixed, grad_tokens, gains, qkv, back, gate, up, down = results
    turned = qkv.shape[0] % 128 != 0
    whole = pl.BlockSpec(memory_space=pltpu.VMEM)
    anywhere = pl.BlockSpec(memory_space=pl.ANY)
    shape = jax.ShapeDtypeStruct
    share, width = qkv.shape[0], mixed.shape[2]

    def facing(array):
        return array.shape if turned else array.shape[::-1]

    out_shape = [
        shape(mixed.shape, BF16),
        shape(grad_tokens.shape, F32),
        shape((1, width), F32),
        shape((1, width), F32),
        shape((1, 256), F32),
        shape((share, 256), F32),
        shape((share, 128), F32),
        shape((share, 128), F32),
        shape(facing(back), F32),
        shape(gate.shape, F32),
        shape(up.shape, F32),
        shape(facing(down), F32),
    ]
    out = pl.pallas_call(
        functools.partial(deliver_kernel, turned),
        out_shape=out_shape,
        in_specs=[anywhere, anywhere, whole] + [anywhere] * 5,
        out_specs=[anywhere, anywhere] + [whole] * 7 + [anywhere, anywhere, whole],
        scratch_shapes=[
            pltpu.VMEM(mixed.shape, BF16),
            pltpu.VMEM(grad_tokens.shape, F32),
            pltpu.VMEM(gate.shape, F32),
            pltpu.VMEM(up.shape, F32),
            pltpu.VMEM(qkv.shape, F32),
            pltpu.VMEM(back.shape, F32),
            pltpu.VMEM(down.shape, F32),
            pltpu.SemaphoreType.DMA((2, 8)),
        ],
        compiler_params=pltpu.CompilerParams(vmem_limit_bytes=32000 * 1024),
        name="deliver_pass",
    )(*results)
    out = list(out)
    if turned:
        out[8], out[11] = out[8].T, out[11].T
    return out


def shards(
    dp_size,
    tokens,
    segment_ids,
    attn_gain,
    query_gain,
    key_gain,
    w_query,
    w_key,
    w_value,
    w_out,
    ffn_gain,
    w_gate,
    w_up,
    w_down,
    cotangent,
):
    own_tokens, own_cot = tokens[:, 0], cotangent[:, 0]
    attn_row, ffn_row = attn_gain[None], ffn_gain[None]
    saved = forward(
        dp_size,
        own_tokens,
        own_cot,
        segment_ids[:, 0],
        (w_query, w_key, w_value, w_out, w_gate, w_up, w_down),
        (attn_row, ffn_row, query_gain[None], key_gain[None]),
    )
    results = backward(dp_size, own_cot, attn_row, ffn_row, own_tokens, saved)
    (
        mixed,
        grad_tokens,
        attn_term,
        ffn_term,
        head_terms,
        grad_query,
        grad_key,
        grad_value,
        grad_out,
        grad_gate,
        grad_up,
        grad_down,
    ) = deliver(results)
    query_term = head_terms[0, :128].reshape(2, DH).sum(0) / query_gain
    key_term = head_terms[0, 128:256].reshape(2, DH).sum(0) / key_gain
    return (
        mixed[:, None],
        grad_tokens[:, None],
        attn_term[0],
        query_term,
        key_term,
        grad_query,
        grad_key,
        grad_value,
        grad_out,
        ffn_term[0],
        grad_gate,
        grad_up,
        grad_down,
    )


def solution(mesh):
    sequence = P(None, "dp", "tensor", None)
    rows = P("dp", "tensor")
    columns = P("tensor", "dp")
    return jax.shard_map(
        functools.partial(shards, mesh.shape["dp"]),
        mesh=mesh,
        in_specs=(sequence, P(None, "dp", None), P(), P(), P(), rows, rows, rows, columns, P(), rows, rows, columns, sequence),
        out_specs=(sequence, sequence, P(), P(), P(), rows, rows, rows, columns, P(), rows, rows, columns),
        check_vma=False,
    )
```

profile of v0, /device:TPU:0, one launch (start us, length us, event | category | flops | bytes accessed | tf_op | source)
XLA Modules:
  0.0 277.7 jit_solution(6485729079965576857)
XLA Ops:
  0.6 1.3 copy.32
  1.9 122.7 %forward_pass.1 = (bf16[1024,512]{1,0:T(8,128)(2,1)}, bf16[1024,256]{1,0:T(8,128)(2,1)}, bf16[1024,1152]{1,0:T(8,128)(2,1)}, bf16[1024,1152]{1,0:T(8,128)(2,1)},...) custom-call(bf16[2,256,1024]{2,1,0:T(8,128)(2,1)} %bitcast.19, ...), custom_call_target="tpu_custom_call" | custom-call | tf_op jit(solution)/shard_map/forward_pass/pallas_call | solution.py:797
  124.6 138.9 %backward_pass.1 = (bf16[2,256,1024]{2,1,0:T(8,128)(2,1)}, f32[2,256,1024]{2,1,0:T(8,128)}, f32[8,384]{1,0:T(8,128)}, f32[128,512]{1,0:T(8,128)}, f32[128,256]{1...) custom-call(bf16[2,256,1024]{2,1,0:T(8,128)(2,1)} %bitcast.18, f32[1,1024]{1,0:T(1,128)} %bitcast.23, ...), custom_call_target="tpu_custom_call" | custom-call | tf_op jit(solution)/shard_map/backward_pass/pallas_call | solution.py:1632
  263.6 0.0 copy-start.8
  263.6 0.0 copy-start.9
  263.6 0.0 copy-start
  263.6 1.6 copy-done
  265.2 0.0 copy-start.1
  265.2 1.2 copy-done.1
  266.4 0.0 copy-start.2
  266.4 1.1 copy-done.2
  267.5 0.0 copy-start.3
  267.5 1.1 copy-done.3
  268.6 0.0 copy-start.4
  268.6 1.1 copy-done.4
  269.6 0.0 copy-start.5
  269.6 0.9 copy-done.5
  270.6 0.0 copy-start.6
  270.6 0.9 copy-done.6
  271.5 0.0 copy-start.7
  271.5 0.7 copy-done.7
  272.2 4.2 %deliver_pass.1 = (bf16[2,256,1024]{2,1,0:T(8,128)(2,1)}, f32[2,256,1024]{2,1,0:T(8,128)}, f32[1,1024]{1,0:T(1,128)}, f32[1,1024]{1,0:T(1,128)}, f32[1,256]{1,0:...) custom-call(bf16[2,256,1024]{2,1,0:T(8,128)(2,1)S(1)} %copy-done.1, ...), custom_call_target="tpu_custom_call" | custom-call | tf_op jit(solution)/shard_map/deliver_pass/pallas_call | solution.py:1740
  276.4 0.1 reshape_squeeze.7
  276.5 0.0 copy-done.8
  276.5 0.5 div.7
  277.0 0.1 reshape_squeeze.6
  277.1 0.0 copy-done.9
  277.1 0.5 div.6
  (3 shorter events, 0.1 us)
Async XLA Ops:
  263.6 12.9 %copy-start.8 = (f32[64]{0:T(128)S(1)}, f32[64]{0:T(128)}, u32[]{:S(2)}) copy-start(f32[64]{0:T(128)} %param.19) | copy-start | bytes 772
  263.6 13.6 %copy-start.9 = (f32[64]{0:T(128)S(1)}, f32[64]{0:T(128)}, u32[]{:S(2)}) copy-start(f32[64]{0:T(128)} %param.18) | copy-start | bytes 772
  263.6 1.6 copy-start
  265.2 1.2 copy-start.1
  266.4 1.1 copy-start.2
  267.5 1.1 copy-start.3
  268.6 1.1 copy-start.4
  269.6 0.9 copy-start.5
  270.6 0.9 copy-start.6
  271.5 0.7 copy-start.7
where the time goes:
time: 278 us
  Pallas kernels  266 us (96%)
  local copies, waits for them, and re-layouts  10.1 us (4%)
    pallas_call x1, Pallas kernels, backward(): pl.pallas_call(functools.partial(backward_kernel, dp_size), out_shape=out...  139 us
    pallas_call x1, Pallas kernels, forward(): pl.pallas_call(functools.partial(forward_kernel, dp_size, turned), out_sh...  123 us
    unnamed x21, local copies, waits for them, and re-layouts  9.88 us

commit v1 on v0

--- a/solution.py
+++ b/solution.py
@@ -207,9 +207,12 @@
             self.staged[half] = values.astype(BF16)
             self.twin(half).start()
         elif step == 1:
-            self.twin(0).wait_recv()
-            self.staged[2] = (values + self.from_twin[0].astype(F32)).astype(BF16)
-            self.crossing().start()
+            self.staged[2] = values.astype(BF16)
+
+    def cross(self):
+        self.twin(0).wait_recv()
+        self.staged[2] = (self.staged[2].astype(F32) + self.from_twin[0].astype(F32)).astype(BF16)
+        self.crossing().start()
 
     def result(self, values):
         self.twin(1).wait_recv()
@@ -262,8 +265,8 @@
             self.shard, self.at(place.dp), self.inner_sems, (self.piece, 0), dp=place.other
         )
 
-    def send_outer(self):
-        @pl.loop(1, self.place.outer_size)
+    def send_outer(self, first, last):
+        @pl.loop(first, last)
         def _(shift):
             self.outer_copy(shift).start()
 
@@ -405,6 +408,10 @@
         saves.append(copy)
         return copy
 
+    def save_columns(src, dst, m):
+        for block in range(dst.shape[0]):
+            save(src.at[m, :, TILE * block : TILE * block + TILE], dst.at[block, m])
+
     lane = lax.broadcasted_iota(jnp.int32, (TILE, 128), 1)
     front = lane < 64
     place_in = rem(lane, 64)
@@ -422,11 +429,25 @@
         back_shard[...] = w_out[...].T
         down_shard[...] = w_down[...].T
     place.greet(False)
-    qkv_w.send_outer()
-    qkv_w.send_inner()
+    cuts = (1, first_cut, second_cut, outer_size)
+    order = (qkv_w, back_w, gate_w, up_w, down_w)
+
+    def issue(item):
+        piece, part = order[item // 3], item % 3
+        piece.send_outer(cuts[part], cuts[part + 1])
+        if part == 0:
+            piece.send_inner()
+
+    def take(item):
+        part = item % 3
+        order[item // 3].relay(cuts[part], cuts[part + 1])
+        for following in {0: (2,), 1: (3, 4), 2: (5, 6), 3: (7,), 4: (), 5: (8,)}.get(item, (item + 3,)):
+            if following < 3 * len(order):
+                issue(following)
+
+    issue(0)
+    issue(1)
     normed_g[0].start()
-    normed_g[1].start()
-    cot_g[0].start()
 
     def prepare():
         fill_mixer(mixer)
@@ -451,7 +472,7 @@
         for m in range(micro_count):
             for block in range(block_count):
                 rows = slice(block * TILE, (block + 1) * TILE)
-                ids = jnp.broadcast_to(segments[m : m + 1, rows], (16, TILE))
+                ids = jnp.broadcast_to(segments[m, :, rows], (16, TILE))
                 match = lax.broadcasted_iota(jnp.int32, (16, TILE), 0) == ids
                 marks = tn(jnp.where(match, 1.0, 0.0).astype(BF16), spread)
                 query_marks[m, rows] = marks.astype(BF16)
@@ -469,14 +490,10 @@
     prepare()
     save(down_shard, down_w.at(place.dp))
     save(tables, out_tables)
-    qkv_w.relay(1, second_cut)
-    back_w.send_outer()
-    qkv_w.relay(second_cut, outer_size)
-    back_w.send_inner()
-    gate_w.send_outer()
-    gate_w.send_inner()
-    up_w.send_outer()
-    down_w.send_outer()
+    take(0)
+    take(1)
+    take(2)
+    normed_g[1].start()
 
     later = lax.broadcasted_iota(jnp.int32, (TILE, TILE), 1) > lax.broadcasted_iota(
         jnp.int32, (TILE, TILE), 0
@@ -573,6 +590,7 @@
         @pl.when(m == 0)
         def _():
             normed_g[0].relay()
+            take(3)
             normed_g[0].finish()
             qkv_w.finish()
 
@@ -584,12 +602,9 @@
 
         @pl.when(m == 0)
         def _():
-            back_w.relay(1, outer_size)
-            up_w.send_inner()
-
-        @pl.when(m == 1)
-        def _():
-            gate_w.relay(1, first_cut)
+            take(4)
+            take(5)
+            cot_g[0].start()
 
         attend(m)
 
@@ -598,11 +613,13 @@
             normed_g[1].relay()
             back_w.finish()
 
-        @pl.when(m == 1)
+        branch(m)
+
+        @pl.when(m == 0)
         def _():
-            down_w.send_inner()
-
-        branch(m)
+            take(6)
+
+        branch_s(m).cross()
 
     save(qkv_full, out_qkv_full)
     save(back_full, out_back_full)
@@ -612,23 +629,23 @@
         save(value.at[m], out_value.at[m])
         save(attended.at[m], out_attended.at[m])
         save(proj.at[m], out_proj.at[m])
-        save(normed.at[m], out_normed.at[m])
-    gate_w.relay(first_cut, second_cut)
+        save_columns(normed, out_normed, m)
+    take(7)
     cot_g[0].relay()
-    gate_w.relay(second_cut, outer_size)
+    take(8)
     enter_ffn(0)
-    up_w.relay(1, first_cut)
+    take(9)
     enter_ffn(1)
-    cot_g[1].start()
-    up_w.relay(first_cut, second_cut)
     cot_g[0].finish()
     save(cot_all.at[0], out_cot.at[0])
     gate_w.finish()
     save(gate_full, out_gate_full)
-    up_w.relay(second_cut, outer_size)
+    take(10)
     ffn_g[0].relay()
+    cot_g[1].start()
+    take(11)
     ffn_g[0].finish()
-    save(ffn_all.at[0], out_ffn.at[0])
+    save_columns(ffn_all, out_ffn, 0)
     up_w.finish()
     save(up_full, out_up_full)
 
@@ -656,18 +673,18 @@
             for copy in slope_copies(index - 2):
                 copy.wait()
 
-        @pl.when(index == 2)
+        @pl.when(index == 1)
         def _():
-            down_w.relay(1, first_cut)
+            take(12)
 
         @pl.when(index == block_count)
         def _():
             ffn_g[1].relay()
             ffn_g[1].finish()
 
-        @pl.when(index == block_count + 2)
+        @pl.when(index == block_count + 3)
         def _():
-            down_w.relay(first_cut, second_cut)
+            take(13)
 
         gate = nn(ffn_all[m, rows], gate_full[...])
         up = nn(ffn_all[m, rows], up_full[...])
@@ -679,13 +696,13 @@
         for copy in slope_copies(index):
             copy.start()
 
-    save(ffn_all.at[1], out_ffn.at[1])
+    save_columns(ffn_all, out_ffn, 1)
     save(hidden, out_hidden)
     for index in (tile_count - 2, tile_count - 1):
         for copy in slope_copies(index):
             copy.wait()
     cot_g[1].relay()
-    down_w.relay(second_cut, outer_size)
+    take(14)
     cot_g[1].finish()
     save(cot_all.at[1], out_cot.at[1])
 
@@ -712,7 +729,7 @@
 def forward(dp_size, tokens, cotangent, segments, weights, gains):
     w_query, w_key, w_value, w_out, w_gate, w_up, w_down = weights
     micro, rows, width = tokens.shape
-    length = segments.shape[1]
+    length = segments.shape[2]
     share, hidden_width = w_gate.shape
     qkv_width = w_query.shape[1] + w_key.shape[1] + w_value.shape[1]
     back_width = w_out.shape[0]
@@ -729,8 +746,8 @@
         shape((width, hidden_width), BF16),
         shape((width, hidden_width), BF16),
         shape((width, hidden_width), BF16),
-        shape((micro, length, width), BF16),
-        shape((micro, length, width), BF16),
+        shape((width // TILE, micro, length, TILE), BF16),
+        shape((width // TILE, micro, length, TILE), BF16),
         shape((micro, length, width), BF16),
         shape((micro, length, hidden_width), BF16),
         shape((micro, length, hidden_width), BF16),
@@ -777,7 +794,7 @@
         pltpu.SemaphoreType.DMA((5, outer_size)),
         pltpu.SemaphoreType.DMA((24,)),
         pltpu.SemaphoreType.DMA((24,)),
-        pltpu.SemaphoreType.DMA((32,)),
+        pltpu.SemaphoreType.DMA((48,)),
         pltpu.SemaphoreType.DMA((2, 2)),
     ]
     operands = (
@@ -847,12 +864,10 @@
             dp=place.ahead(shift),
         )
 
-    def give(self):
-        @pl.loop(1, self.place.outer_size)
+    def give(self, first, last):
+        @pl.loop(first, last)
         def _(shift):
             self.inner_copy(shift).start()
-
-        self.inner_copy(0).start()
 
     def turn(self, first, last):
         @pl.loop(first, last)
@@ -999,11 +1014,13 @@
     def turn_block(step):
         return rem(step + 1 + own_outer_block, 4)
 
-    def give_block(share, block):
-        @pl.loop(0, outers)
-        def _(index):
-            shift = rem(block * outers + index - place.outer + outer_size, outer_size)
-            share.inner_copy(shift).start()
+    cuts = (1, first_cut, second_cut, outer_size)
+
+    def issue(share, part):
+        share.give(*((0, 1) if part == 3 else (cuts[part], cuts[part + 1])))
+
+    def take(share, part):
+        share.turn(cuts[part], cuts[part + 1])
 
     def twin_copy(kind, m, half):
         from_twin = (part_twin, out_twin, part_twin)[kind]
@@ -1030,24 +1047,19 @@
         core = jnp.where(rem(step, 2) == 0, 1 - place.core, place.core)
         return side * 2 + core
 
-    def hand_out(kind, m, step, values):
-        from_twin = (part_twin, out_twin, part_twin)[kind]
-        half = step // 2
-
+    def hand_out(m, step, values):
+        staged[m, rem(step, 2) * 2 + step // 2] = values.astype(BF16)
+
+    def send_twin(kind, m, step):
         @pl.when(rem(step, 2) == 0)
         def _():
-            staged[m, half] = values.astype(BF16)
-            twin_copy(kind, m, half).start()
-
-        @pl.when(step == 1)
-        def _():
-            twin_copy(kind, m, 0).wait_recv()
-            staged[m, 2] = (values + from_twin[m, 0].astype(F32)).astype(BF16)
-            across_copy(kind, m).start()
-
-        @pl.when(step == 3)
-        def _():
-            staged[m, 3] = values.astype(BF16)
+            twin_copy(kind, m, step // 2).start()
+
+    def cross(kind, m):
+        from_twin = (part_twin, out_twin, part_twin)[kind]
+        twin_copy(kind, m, 0).wait_recv()
+        staged[m, 2] = (staged[m, 2].astype(F32) + from_twin[m, 0].astype(F32)).astype(BF16)
+        across_copy(kind, m).start()
 
     def collect(kind, m):
         from_twin = (part_twin, out_twin, part_twin)[kind]
@@ -1086,47 +1098,37 @@
             for index, (src, dst) in enumerate(pairs)
         ]
 
-    def ffn_phase(grads, rows_buf, hidden_buf, ffn_cols):
+    def rows_of(index):
+        return index // block_count, tile(block_of(rem(index, block_count)))
+
+    def ffn_phase(grads, rows_buf, ffn_cols):
         def rows_copy(index):
-            m = index // block_count
-            rows = tile(block_of(rem(index, block_count)))
+            m, rows = rows_of(index)
             slot = rem(index, 2)
             return pltpu.make_async_copy(cot_all.at[m, rows], rows_buf.at[slot], tile_sems.at[0, slot])
-
-        def hidden_copy(index):
-            m = index // block_count
-            rows = tile(block_of(rem(index, block_count)))
-            slot = rem(index, 2)
-            return pltpu.make_async_copy(hidden.at[m, rows], hidden_buf.at[slot], tile_sems.at[1, slot])
 
         def cols_copy(index):
             slot = rem(index, 2)
             return pltpu.make_async_copy(
-                ffn_all.at[:, :, tile(turn_block(rem(index, block_count)))],
-                ffn_cols.at[slot],
-                tile_sems.at[2, slot],
+                ffn_all.at[turn_block(rem(index, block_count))], ffn_cols.at[slot], tile_sems.at[2, slot]
             )
 
         loads = [load(down_full, down_w)]
         rows_copy(0).start()
         loads += [load(gate_slope.at[0], grads.at[0, 0]), load(up_slope.at[0], grads.at[1, 0])]
-        loads += [load(gate_full, ffn_w.at[0]), load(up_full, ffn_w.at[1]), load(middle_in, middle)]
-        loads.append(load(cotangent, mixed))
-
-        def second_copies():
-            return [
-                pltpu.make_async_copy(slope.at[1], grads.at[kind, 1], local_sems.at[38 + kind])
-                for kind, slope in enumerate((gate_slope, up_slope))
-            ]
+        loads += [load(gate_full, ffn_w.at[0]), load(up_full, ffn_w.at[1])]
+        others = [
+            load(gate_slope.at[1], grads.at[0, 1]),
+            load(up_slope.at[1], grads.at[1, 1]),
+            load(middle_in, middle),
+            load(cotangent, mixed),
+        ]
 
         def kept_copy(shift):
             return pltpu.make_async_copy(
                 down_s.at(place.ahead(shift)), down_kept.at[shift], local_sems.at[40 + shift]
             )
 
-        for copy in second_copies():
-            copy.start()
-
         @pl.loop(0, outer_size)
         def _(shift):
             kept_copy(shift).start()
@@ -1135,20 +1137,25 @@
         gain_parts[...] = jnp.zeros_like(gain_parts)
         gain_packed[...] = jnp.zeros_like(gain_packed)
         place.greet(True)
-        down_s.give()
+        issue(down_s, 0)
+        issue(down_s, 1)
         for copy in loads:
             copy.wait()
 
         @pl.loop(0, tile_count)
         def _(index):
-            m = index // block_count
+            m, rows = rows_of(index)
             step = rem(index, block_count)
-            rows = tile(block_of(step))
             slot = rem(index, 2)
 
             @pl.when(index + 1 < tile_count)
             def _():
                 rows_copy(index + 1).start()
+
+            @pl.when(index == block_count)
+            def _():
+                pltpu.make_async_copy(gate_slope.at[1], grads.at[0, 1], local_sems.at[5]).wait()
+                pltpu.make_async_copy(up_slope.at[1], grads.at[1, 1], local_sems.at[6]).wait()
 
             @pl.when(index == 2)
             def _():
@@ -1156,21 +1163,13 @@
                 def _(shift):
                     kept_copy(shift).wait()
 
-                down_s.turn(1, first_cut)
-
-            @pl.when(index == block_count)
-            def _():
-                for copy in second_copies():
-                    copy.wait()
+                take(down_s, 0)
+                issue(down_s, 2)
 
             @pl.when(index == block_count + 1)
             def _():
-                down_s.turn(first_cut, second_cut)
-
-            @pl.when(index == block_count + 3)
-            def _():
-                down_s.turn(second_cut, outer_size)
-                leave_ffn(0)
+                take(down_s, 1)
+                issue(down_s, 3)
 
             rows_copy(index).wait()
             hidden_grad = nn(rows_buf[slot], down_w[...])
@@ -1178,11 +1177,21 @@
             up_low = (hidden_grad * grads[1, m, rows].astype(F32)).astype(BF16)
             grads[0, m, rows] = gate_low
             grads[1, m, rows] = up_low
-            hand_out(0, m, step, nt(gate_low, ffn_w[0]) + nt(up_low, ffn_w[1]))
+            hand_out(m, step, nt(gate_low, ffn_w[0]) + nt(up_low, ffn_w[1]))
+
+            send_twin(0, m, step)
+
+            @pl.when(index == 2)
+            def _():
+                cross(0, 0)
 
         for copy in attn_copies():
             copy.start()
         cols_copy(0).start()
+        for copy in others[2:]:
+            copy.wait()
+        leave_ffn(0)
+        cross(0, 1)
 
         @pl.loop(0, 2 * block_count)
         def _(index):
@@ -1198,43 +1207,35 @@
             ffn_w[kind, tile(block)] = (
                 tn(ffn_cols[slot, 0], grads[kind, 0]) + tn(ffn_cols[slot, 1], grads[kind, 1])
             ).astype(BF16)
-            give_block(ffn_shares(kind), block)
-
-            @pl.when(index == block_count + 2)
+
+            @pl.when(index == 1)
             def _():
-                leave_ffn(1)
-
-        hidden_copy(0).start()
-
-        @pl.loop(0, tile_count)
-        def _(index):
-            m = index // block_count
-            step = rem(index, block_count)
-            slot = rem(index, 2)
-
-            @pl.when(index + 1 < tile_count)
+                take(down_s, 2)
+                if outers == 1:
+                    issue(gate_s, 0)
+
+            @pl.when(index == block_count - 1)
             def _():
-                hidden_copy(index + 1).start()
-
-            hidden_copy(index).wait()
-
-            @pl.when(step == 0)
+                if outers > 1:
+                    issue(gate_s, 0)
+                issue(gate_s, 1)
+
+            @pl.when(index == block_count + 3)
             def _():
-                drain(0, m)
-
-            hand_out(1, m, step, nt(hidden_buf[slot], down_w[...]))
+                take(gate_s, 0)
+                issue(gate_s, 2)
 
     pl.run_scoped(
         ffn_phase,
         pltpu.VMEM((2, micro_count, length, hidden_width), BF16),
         pltpu.VMEM((2, TILE, width), BF16),
-        pltpu.VMEM((2, TILE, hidden_width), BF16),
         pltpu.VMEM((2, micro_count, length, TILE), BF16),
     )
 
     def attn_phase(
         toks,
         tabs,
+        hidden_buf,
         grad_att,
         grad_q,
         grad_k,
@@ -1326,9 +1327,7 @@
                     grad_k[group, rows] = both_k + pltpu.roll(both_k, 64, 1)
                     grad_v[group, rows] = both_v + pltpu.roll(both_v, 64, 1)
 
-                @pl.when(group == 0)
-                def _():
-                    between()
+                between(group)
 
         def normalize_back(grads, values, cosine, sine):
             scaled = grads * LN2
@@ -1367,7 +1366,10 @@
             @pl.loop(0, block_count)
             def _(step):
                 rows = tile(block_of(step))
-                hand_out(2, m, step, nt(grad_qkv[m, rows], qkv_w[:, 0:512]))
+                hand_out(m, step, nt(grad_qkv[m, rows], qkv_w[:, 0:512]))
+                send_twin(2, m, step)
+
+            cross(2, m)
 
         def leave_attn(m):
             upstream = collect(2, m)
@@ -1375,11 +1377,13 @@
             middle[m] = mid_all[m, own].astype(F32) + back
             gain_parts[0:1, :] += term
 
-        def norm_copy(index):
-            slot = rem(index, 2)
-            return pltpu.make_async_copy(
-                normed.at[:, :, tile(turn_block(index))], val.at[slot], tile_sems.at[3, slot]
-            )
+        def norm_copies():
+            return [
+                pltpu.make_async_copy(
+                    normed.at[turn_block(step)], norm_cols.at[step % 2], local_sems.at[24 + step]
+                )
+                for step, norm_cols in enumerate((ky, ky, val, val))
+            ]
 
         reloads = ((value, val), (key, ky), (query, qry), (proj, prj))
 
@@ -1400,48 +1404,84 @@
                     heads = jnp.concatenate([att[m, 0], att[m, 1]], axis=1)
                     total = total + tn(mid_all[m, :, columns], heads)
                 back_part[columns] = total.astype(BF16)
-                give_block(back_s, block)
-
-        table_load.wait()
-        token_load.wait()
+
+        def hidden_copy(index):
+            m, rows = rows_of(index)
+            slot = rem(index, block_count)
+            return pltpu.make_async_copy(
+                hidden.at[m, rows], hidden_buf.at[slot], local_sems.at[24 + slot]
+            )
+
+        def enter_out():
+            for m in range(micro_count):
+                drain(0, m)
+
+            @pl.loop(0, tile_count)
+            def _(index):
+                m = index // block_count
+                step = rem(index, block_count)
+                hidden_copy(index).wait()
+                hand_out(m, step, nt(hidden_buf[step], down_w[...]))
+                send_twin(1, m, step)
+
+                @pl.when(index + block_count < tile_count)
+                def _():
+                    hidden_copy(index + block_count).start()
+
+                @pl.when(index == block_count)
+                def _():
+                    take(up_s, 0)
+                    issue(up_s, 2)
+
+        for slot in range(block_count):
+            hidden_copy(slot).start()
+        for copy in attn_copies():
+            copy.wait()
+        down_s.keep(down_total)
+        mid_g[0].relay()
+        mid_g[0].finish()
 
         @pl.loop(0, micro_count)
         def _(m):
+            score_ready(m)
+
             @pl.when(m == 0)
             def _():
-                down_s.keep(down_total)
-                gate_s.turn(1, first_cut)
-                mid_g[0].relay()
-                for copy in attn_copies():
-                    copy.wait()
-                mid_g[0].finish()
+                take(gate_s, 1)
+                issue(gate_s, 3)
 
             @pl.when(m == 1)
             def _():
-                mid_g[1].finish()
-                for index in range(4):
-                    reload_copy(index).wait()
-
-            score_ready(m)
-
-            @pl.when(m == 0)
-            def _():
-                gate_s.turn(first_cut, second_cut)
-
-            @pl.when(m == 1)
-            def _():
+                take(up_s, 1)
+                issue(up_s, 3)
                 enter_back()
-                up_s.turn(first_cut, second_cut)
-
-            def between():
-                @pl.when(m == 0)
+
+            def between(group):
+                @pl.when((m == 0) & (group == 0))
                 def _():
-                    gate_s.turn(second_cut, outer_size)
-                    mid_g[1].relay()
-
-                @pl.when(m == 1)
+                    take(gate_s, 2)
+                    issue(up_s, 0)
+                    leave_ffn(1)
+
+                @pl.when((m == 0) & (group == 1))
                 def _():
-                    up_s.turn(second_cut, outer_size)
+                    gate_s.keep(gate_total)
+                    issue(up_s, 1)
+
+                @pl.when((m == 1) & (group == 0))
+                def _():
+                    take(up_s, 2)
+                    issue(back_s, 0)
+                    issue(back_s, 1)
+                    leave_out(0)
+                    mixed_save(0).start()
+                    enter_norm(0)
+
+                @pl.when((m == 1) & (group == 1))
+                def _():
+                    up_s.keep(up_total)
+                    issue(back_s, 2)
+                    issue(back_s, 3)
 
             attend_back(m, between)
 
@@ -1449,56 +1489,60 @@
             def _():
                 for index in range(3):
                     reload_copy(index).start()
-                gate_s.keep(gate_total)
+                table_load.wait()
 
             @pl.when(m == 1)
             def _():
-                norm_copy(0).start()
+                for copy in norm_copies():
+                    copy.start()
 
             leave_heads(m)
 
             @pl.when(m == 0)
             def _():
                 reload_copy(3).start()
-                up_s.turn(1, first_cut)
-
-            @pl.when(m == 1)
-            def _():
-                up_s.keep(up_total)
-
-            leave_out(m)
-            mixed_save(m).start()
-            enter_norm(m)
-
+                enter_out()
+                mid_g[1].relay()
+                cross(1, 0)
+                cross(1, 1)
+                mid_g[1].finish()
+                for index in range(4):
+                    reload_copy(index).wait()
+
+        leave_out(1)
+        mixed_save(1).start()
+        enter_norm(1)
+        token_load.wait()
         saves = [mixed_save(m) for m in range(micro_count)]
         down_s.finish(down_total)
         saves.append(load(down_total, out_down))
         gate_s.finish(gate_total)
         saves.append(load(gate_total, out_gate))
-        back_s.turn(1, outer_size)
-
-        @pl.loop(0, block_count)
-        def _(step):
-            block = turn_block(step)
-            columns = tile(block)
-            slot = rem(step, 2)
-            norm_copy(step).wait()
-
-            @pl.when(step + 1 < block_count)
-            def _():
-                norm_copy(step + 1).start()
-
-            qkv_part[columns] = (
-                tn(val[slot, 0], grad_qkv[0]) + tn(val[slot, 1], grad_qkv[1])
-            ).astype(BF16)
-            give_block(qkv_s, block)
-
-        back_s.keep(back_total)
+
+        for half, norm_cols in enumerate((ky, val)):
+
+            @pl.loop(2 * half, 2 * half + 2)
+            def _(step):
+                slot = step - 2 * half
+                pltpu.make_async_copy(
+                    normed.at[turn_block(step)], norm_cols.at[slot], local_sems.at[24 + step]
+                ).wait()
+                qkv_part[tile(turn_block(step))] = (
+                    tn(norm_cols[slot, 0], grad_qkv[0]) + tn(norm_cols[slot, 1], grad_qkv[1])
+                ).astype(BF16)
+                if outers == 1:
+                    qkv_s.inner_copy(rem(step + 1, outer_size)).start()
+
+        if outers > 1:
+            for part in range(4):
+                issue(qkv_s, part)
+        for part in range(3):
+            take(back_s, part)
         leave_attn(0)
         saves.append(load(middle.at[0], out_tokens.at[0]))
-        qkv_s.turn(1, outer_size)
-        up_s.finish(up_total)
-        saves.append(load(up_total, out_up))
+        back_s.keep(back_total)
+        for part in range(3):
+            take(qkv_s, part)
         leave_attn(1)
         saves.append(load(middle.at[1], out_tokens.at[1]))
 
@@ -1515,6 +1559,8 @@
         for shift in range(1, 4):
             group_gain(shift).start()
         qkv_s.keep(qkv_total)
+        up_s.finish(up_total)
+        saves.append(load(up_total, out_up))
         back_s.finish(back_total)
         saves.append(load(back_total, out_back))
         for shift in range(1, 4):
@@ -1559,6 +1605,7 @@
         attn_phase,
         pltpu.VMEM(tokens.shape, BF16),
         pltpu.VMEM(tables.shape, F32),
+        pltpu.VMEM((block_count, TILE, hidden_width), BF16),
         pltpu.VMEM((2, length, 256), BF16),
         pltpu.VMEM((2, length, 128), F32),
         pltpu.VMEM((2, length, 128), F32),
@@ -1578,7 +1625,7 @@
 
 def backward(dp_size, cotangent, attn_gain, ffn_gain, tokens, saved):
     micro, rows, width = tokens.shape
-    length = saved[5].shape[1]
+    length = saved[7].shape[1]
     hidden_width = saved[2].shape[1]
     outer_size = dp_size // 2
     share = width // dp_size
@@ -1647,6 +1694,8 @@
     in_mixed,
     in_tokens,
     gains,
+    query_gain,
+    key_gain,
     in_qkv,
     in_back,
     in_gate,
@@ -1656,7 +1705,8 @@
     grad_tokens,
     attn_gain,
     ffn_gain,
-    head_gains,
+    query_term,
+    key_term,
     grad_query,
     grad_key,
     grad_value,
@@ -1690,12 +1740,16 @@
     for copy in arrivals:
         copy.start()
     part = 0
-    for out in (attn_gain, ffn_gain, head_gains):
+    for out in (attn_gain, ffn_gain):
         for start in range(0, out.shape[1], 128):
             out[:, start : start + 128] = gains[
                 part // 3 : part // 3 + 1, 128 * (part % 3) : 128 * (part % 3) + 128
             ]
             part += 1
+    for out, gain in ((query_term, query_gain), (key_term, key_gain)):
+        term = gains[part // 3 : part // 3 + 1, 128 * (part % 3) : 128 * (part % 3) + 128]
+        out[...] = term[:, :DH] / gain[...] + term[:, DH:] / gain[...]
+        part += 1
     for index, (_, buf, dst) in enumerate(flows):
         arrivals[index].wait()
         if dst is not None:
@@ -1712,11 +1766,12 @@
         copy.wait()
 
 
-def deliver(results):
+def deliver(results, query_gain, key_gain):
     mixed, grad_tokens, gains, qkv, back, gate, up, down = results
     turned = qkv.shape[0] % 128 != 0
     whole = pl.BlockSpec(memory_space=pltpu.VMEM)
     anywhere = pl.BlockSpec(memory_space=pl.ANY)
+    stored = pl.BlockSpec(memory_space=pltpu.HBM)
     shape = jax.ShapeDtypeStruct
     share, width = qkv.shape[0], mixed.shape[2]
 
@@ -1728,7 +1783,8 @@
         shape(grad_tokens.shape, F32),
         shape((1, width), F32),
         shape((1, width), F32),
-        shape((1, 256), F32),
+        shape((1, DH), F32),
+        shape((1, DH), F32),
         shape((share, 256), F32),
         shape((share, 128), F32),
         shape((share, 128), F32),
@@ -1740,8 +1796,8 @@
     out = pl.pallas_call(
         functools.partial(deliver_kernel, turned),
         out_shape=out_shape,
-        in_specs=[anywhere, anywhere, whole] + [anywhere] * 5,
-        out_specs=[anywhere, anywhere] + [whole] * 7 + [anywhere, anywhere, whole],
+        in_specs=[stored, stored] + [whole] * 3 + [stored] * 5,
+        out_specs=[anywhere, anywhere] + [whole] * 8 + [anywhere, anywhere, whole],
         scratch_shapes=[
             pltpu.VMEM(mixed.shape, BF16),
             pltpu.VMEM(grad_tokens.shape, F32),
@@ -1752,12 +1808,12 @@
             pltpu.VMEM(down.shape, F32),
             pltpu.SemaphoreType.DMA((2, 8)),
         ],
-        compiler_params=pltpu.CompilerParams(vmem_limit_bytes=32000 * 1024),
+        compiler_params=pltpu.CompilerParams(vmem_limit_bytes=VMEM_LIMIT),
         name="deliver_pass",
-    )(*results)
+    )(mixed, grad_tokens, gains, query_gain, key_gain, qkv, back, gate, up, down)
     out = list(out)
     if turned:
-        out[8], out[11] = out[8].T, out[11].T
+        out[9], out[12] = out[9].T, out[12].T
     return out
 
 
@@ -1784,7 +1840,7 @@
         dp_size,
         own_tokens,
         own_cot,
-        segment_ids[:, 0],
+        segment_ids,
         (w_query, w_key, w_value, w_out, w_gate, w_up, w_down),
         (attn_row, ffn_row, query_gain[None], key_gain[None]),
     )
@@ -1794,7 +1850,8 @@
         grad_tokens,
         attn_term,
         ffn_term,
-        head_terms,
+        query_term,
+        key_term,
         grad_query,
         grad_key,
         grad_value,
@@ -1802,15 +1859,13 @@
         grad_gate,
         grad_up,
         grad_down,
-    ) = deliver(results)
-    query_term = head_terms[0, :128].reshape(2, DH).sum(0) / query_gain
-    key_term = head_terms[0, 128:256].reshape(2, DH).sum(0) / key_gain
+    ) = deliver(results, query_gain[None], key_gain[None])
     return (
         mixed[:, None],
         grad_tokens[:, None],
         attn_term[0],
-        query_term,
-        key_term,
+        query_term[0],
+        key_term[0],
         grad_query,
         grad_key,
         grad_value,

time: 278 us -> 258 us (0.928)
  local copies, waits for them, and re-layouts: 10.1 us -> 0 us
  Pallas kernels: 266 us -> 257 us
    pallas_call x1, Pallas kernels: 139 us -> 129 us  [backward(): pl.pallas_call(functools.partial(backward_kernel, dp_size), out_shape=out...]
    unnamed x21 -> x0, local copies, waits for them, and re-layouts: 9.88 us -> none
where the time goes in v1:
time: 258 us
  Pallas kernels  257 us (100%)
    pallas_call x1, Pallas kernels, backward(): pl.pallas_call(functools.partial(backward_kernel, dp_size), out_shape=out...  129 us
    pallas_call x1, Pallas kernels, forward(): pl.pallas_call(functools.partial(forward_kernel, dp_size, turned), out_sh...  123 us
    pallas_call x1, Pallas kernels, deliver(): pl.pallas_call(functools.partial(deliver_kernel, turned), out_shape=out_s...  5.44 us

profile of v1, /device:TPU:0, one launch (start us, length us, event | category | flops | bytes accessed | tf_op | source)
XLA Modules:
  0.0 257.8 jit_solution(1988719933746169076)
XLA Ops:
  0.6 122.6 %forward_pass.1 = (bf16[1024,512]{1,0:T(8,128)(2,1)}, bf16[1024,256]{1,0:T(8,128)(2,1)}, bf16[1024,1152]{1,0:T(8,128)(2,1)}, bf16[1024,1152]{1,0:T(8,128)(2,1)},...) custom-call(bf16[2,256,1024]{2,1,0:T(8,128)(2,1)} %bitcast.18, ...), custom_call_target="tpu_custom_call" | custom-call | tf_op jit(solution)/shard_map/forward_pass/pallas_call | solution.py:814
  123.3 128.9 %backward_pass.1 = (bf16[2,256,1024]{2,1,0:T(8,128)(2,1)}, f32[2,256,1024]{2,1,0:T(8,128)}, f32[8,384]{1,0:T(8,128)}, f32[128,512]{1,0:T(8,128)}, f32[128,256]{1...) custom-call(bf16[2,256,1024]{2,1,0:T(8,128)(2,1)} %bitcast.17, f32[1,1024]{1,0:T(1,128)} %bitcast.21, ...), custom_call_target="tpu_custom_call" | custom-call | tf_op jit(solution)/shard_map/backward_pass/pallas_call | solution.py:1679
  252.2 5.4 %deliver_pass.1 = (bf16[2,256,1024]{2,1,0:T(8,128)(2,1)}, f32[2,256,1024]{2,1,0:T(8,128)}, f32[1,1024]{1,0:T(1,128)}, f32[1,1024]{1,0:T(1,128)}, f32[1,64]{1,0:T...) custom-call(bf16[2,256,1024]{2,1,0:T(8,128)(2,1)} %get-tuple-element, ...), custom_call_target="tpu_custom_call" | custom-call | tf_op jit(solution)/shard_map/deliver_pass/pallas_call | solution.py:1796

commit v2 on v1

--- a/solution.py
+++ b/solution.py
@@ -244,53 +244,84 @@
     def at(self, index):
         return self.full.at[pl.ds(pl.multiple_of(index * self.rows, self.rows), self.rows), :]
 
-    def outer_copy(self, shift):
+    def hop(self, way, distance, own=False):
         place = self.place
+        step = 1 - 2 * way
+        rows = self.at((place.outer - step * (distance - 1)) * 2 + place.inner)
         return place.copy(
-            self.shard,
-            self.at(place.dp),
+            self.shard if own else rows,
+            rows,
             self.outer_sems,
-            (self.piece, shift),
-            dp=place.ahead(shift),
+            (self.piece, way, distance),
+            dp=(place.outer + step) * 2 + place.inner,
         )
 
-    def inner_copy(self, shift):
+    def inner_copy(self, source, own=False):
         place = self.place
-        rows = self.at(place.behind(shift))
-        return place.copy(rows, rows, self.inner_sems, (self.piece, shift), dp=place.other)
-
-    def own_copy(self):
+        rows = self.at(source * 2 + place.inner)
+        return place.copy(
+            self.shard if own else rows,
+            rows,
+            self.inner_sems,
+            (self.piece, source),
+            dp=place.other,
+        )
+
+    def arrival(self, way, distance):
         place = self.place
+        rows = self.at(place.dp)
         return place.copy(
-            self.shard, self.at(place.dp), self.inner_sems, (self.piece, 0), dp=place.other
+            rows, rows, self.outer_sems, (self.piece, way, distance), dp=place.other
         )
 
-    def send_outer(self, first, last):
+    def goes(self, way):
+        place = self.place
+        return place.outer > 0 if way else place.outer + 1 < place.outer_size
+
+    def begin(self):
+        for way in range(2):
+
+            @pl.when(self.goes(way))
+            def _():
+                self.hop(way, 1, own=True).start()
+
+        self.inner_copy(self.place.outer, own=True).start()
+
+    def relay(self, first, last):
+        place = self.place
+
         @pl.loop(first, last)
-        def _(shift):
-            self.outer_copy(shift).start()
-
-    def send_inner(self):
-        self.own_copy().start()
-
-    def relay(self, first, last):
-        @pl.loop(first, last)
-        def _(shift):
-            self.outer_copy(shift).wait_recv()
-            self.inner_copy(shift).start()
+        def _(distance):
+            for way in range(2):
+                source = place.outer + distance if way else place.outer - distance
+
+                @pl.when((source >= 0) & (source < place.outer_size))
+                def _():
+                    self.arrival(way, distance).wait_recv()
+
+                    @pl.when(self.goes(way))
+                    def _():
+                        self.hop(way, distance + 1).start()
+
+                    self.inner_copy(source).start()
 
     def finish(self):
         @pl.loop(0, self.place.outer_size)
-        def _(shift):
-            self.inner_copy(shift).wait_recv()
+        def _(source):
+            self.inner_copy(source).wait_recv()
 
     def drain(self):
-        self.own_copy().wait_send()
-
-        @pl.loop(1, self.place.outer_size)
-        def _(shift):
-            self.outer_copy(shift).wait_send()
-            self.inner_copy(shift).wait_send()
+        place = self.place
+
+        @pl.loop(0, place.outer_size)
+        def _(source):
+            self.inner_copy(source).wait_send()
+            for way in range(2):
+                distance = source - place.outer + 1 if way else place.outer - source + 1
+
+                @pl.when(self.goes(way) & (distance >= 1))
+                def _():
+                    self.hop(way, distance).wait_send()
 
 
 def rotation_angles(length):
@@ -432,21 +463,11 @@
     cuts = (1, first_cut, second_cut, outer_size)
     order = (qkv_w, back_w, gate_w, up_w, down_w)
 
-    def issue(item):
-        piece, part = order[item // 3], item % 3
-        piece.send_outer(cuts[part], cuts[part + 1])
-        if part == 0:
-            piece.send_inner()
-
     def take(item):
         part = item % 3
         order[item // 3].relay(cuts[part], cuts[part + 1])
-        for following in {0: (2,), 1: (3, 4), 2: (5, 6), 3: (7,), 4: (), 5: (8,)}.get(item, (item + 3,)):
-            if following < 3 * len(order):
-                issue(following)
-
-    issue(0)
-    issue(1)
+
+    qkv_w.begin()
     normed_g[0].start()
 
     def prepare():
@@ -491,9 +512,12 @@
     save(down_shard, down_w.at(place.dp))
     save(tables, out_tables)
     take(0)
+    back_w.begin()
     take(1)
+    normed_g[1].start()
     take(2)
-    normed_g[1].start()
+    take(3)
+    gate_w.begin()
 
     later = lax.broadcasted_iota(jnp.int32, (TILE, TILE), 1) > lax.broadcasted_iota(
         jnp.int32, (TILE, TILE), 0
@@ -590,7 +614,7 @@
         @pl.when(m == 0)
         def _():
             normed_g[0].relay()
-            take(3)
+            take(4)
             normed_g[0].finish()
             qkv_w.finish()
 
@@ -602,7 +626,6 @@
 
         @pl.when(m == 0)
         def _():
-            take(4)
             take(5)
             cot_g[0].start()
 
@@ -620,6 +643,15 @@
             take(6)
 
         branch_s(m).cross()
+
+        @pl.when(m == 0)
+        def _():
+            take(7)
+
+        @pl.when(m == 1)
+        def _():
+            take(8)
+            up_w.begin()
 
     save(qkv_full, out_qkv_full)
     save(back_full, out_back_full)
@@ -630,22 +662,38 @@
         save(attended.at[m], out_attended.at[m])
         save(proj.at[m], out_proj.at[m])
         save_columns(normed, out_normed, m)
-    take(7)
     cot_g[0].relay()
-    take(8)
     enter_ffn(0)
     take(9)
     enter_ffn(1)
+    take(10)
+    gate_w.finish()
+    save(gate_full, out_gate_full)
+    take(11)
+    down_w.begin()
     cot_g[0].finish()
     save(cot_all.at[0], out_cot.at[0])
-    gate_w.finish()
-    save(gate_full, out_gate_full)
-    take(10)
     ffn_g[0].relay()
     cot_g[1].start()
-    take(11)
     ffn_g[0].finish()
     save_columns(ffn_all, out_ffn, 0)
+    tile_count = micro_count * block_count
+
+    @pl.loop(0, tile_count)
+    def _(index):
+        m = index // block_count
+        rows = tile(rem(index, block_count))
+
+        @pl.when(index == block_count)
+        def _():
+            take(12)
+            ffn_g[1].relay()
+            ffn_g[1].finish()
+
+        hidden[m, rows] = nn(ffn_all[m, rows], gate_full[...]).astype(BF16)
+
+    take(13)
+    save_columns(ffn_all, out_ffn, 1)
     up_w.finish()
     save(up_full, out_up_full)
 
@@ -660,8 +708,6 @@
             for kind, out in enumerate((out_gate_slope, out_up_slope))
         ]
 
-    tile_count = micro_count * block_count
-
     @pl.loop(0, tile_count)
     def _(index):
         m = index // block_count
@@ -673,20 +719,7 @@
             for copy in slope_copies(index - 2):
                 copy.wait()
 
-        @pl.when(index == 1)
-        def _():
-            take(12)
-
-        @pl.when(index == block_count)
-        def _():
-            ffn_g[1].relay()
-            ffn_g[1].finish()
-
-        @pl.when(index == block_count + 3)
-        def _():
-            take(13)
-
-        gate = nn(ffn_all[m, rows], gate_full[...])
+        gate = hidden[m, rows].astype(F32)
         up = nn(ffn_all[m, rows], up_full[...])
         sig = 1.0 / (1.0 + jnp.exp(-gate))
         act = gate * sig
@@ -696,13 +729,18 @@
         for copy in slope_copies(index):
             copy.start()
 
-    save_columns(ffn_all, out_ffn, 1)
     save(hidden, out_hidden)
     for index in (tile_count - 2, tile_count - 1):
         for copy in slope_copies(index):
             copy.wait()
+    take(14)
+
+    @pl.loop(0, block_count)
+    def _(block):
+        columns = tile(block)
+        grad_down[columns] = tn(cot_all[0, :, columns], hidden[0]).astype(BF16)
+
     cot_g[1].relay()
-    take(14)
     cot_g[1].finish()
     save(cot_all.at[1], out_cot.at[1])
 
@@ -710,7 +748,7 @@
     def _(block):
         columns = tile(block)
         grad_down[columns] = (
-            tn(cot_all[0, :, columns], hidden[0]) + tn(cot_all[1, :, columns], hidden[1])
+            grad_down[columns].astype(F32) + tn(cot_all[1, :, columns], hidden[1])
         ).astype(BF16)
 
     save(grad_down, out_grad_down)
@@ -788,8 +826,8 @@
         pltpu.VMEM((micro, 3, rows, width), BF16),
         pltpu.VMEM((micro, 2, rows, width), BF16),
         pltpu.VMEM((micro, rows, width), BF16),
-        pltpu.SemaphoreType.DMA((5, outer_size)),
-        pltpu.SemaphoreType.DMA((5, outer_size)),
+        pltpu.SemaphoreType.DMA((5, 2, outer_size)),
+        pltpu.SemaphoreType.DMA((5, 2, outer_size)),
         pltpu.SemaphoreType.DMA((5, outer_size)),
         pltpu.SemaphoreType.DMA((5, outer_size)),
         pltpu.SemaphoreType.DMA((24,)),
@@ -1413,13 +1451,20 @@
             )
 
         def enter_out():
-            for m in range(micro_count):
-                drain(0, m)
+            drain(0, 0)
 
             @pl.loop(0, tile_count)
             def _(index):
                 m = index // block_count
                 step = rem(index, block_count)
+
+                @pl.when(index == block_count)
+                def _():
+                    take(gate_s, 1)
+                    issue(gate_s, 3)
+                    leave_ffn(1)
+                    drain(0, 1)
+
                 hidden_copy(index).wait()
                 hand_out(m, step, nt(hidden_buf[step], down_w[...]))
                 send_twin(1, m, step)
@@ -1427,11 +1472,6 @@
                 @pl.when(index + block_count < tile_count)
                 def _():
                     hidden_copy(index + block_count).start()
-
-                @pl.when(index == block_count)
-                def _():
-                    take(up_s, 0)
-                    issue(up_s, 2)
 
         for slot in range(block_count):
             hidden_copy(slot).start()
@@ -1439,19 +1479,19 @@
             copy.wait()
         down_s.keep(down_total)
         mid_g[0].relay()
+        enter_out()
+        cross(1, 0)
         mid_g[0].finish()
 
         @pl.loop(0, micro_count)
         def _(m):
             score_ready(m)
 
-            @pl.when(m == 0)
-            def _():
-                take(gate_s, 1)
-                issue(gate_s, 3)
-
             @pl.when(m == 1)
             def _():
+                leave_out(0)
+                mixed_save(0).start()
+                enter_norm(0)
                 take(up_s, 1)
                 issue(up_s, 3)
                 enter_back()
@@ -1461,21 +1501,19 @@
                 def _():
                     take(gate_s, 2)
                     issue(up_s, 0)
-                    leave_ffn(1)
 
                 @pl.when((m == 0) & (group == 1))
                 def _():
                     gate_s.keep(gate_total)
                     issue(up_s, 1)
+                    cross(1, 1)
+                    mid_g[1].relay()
 
                 @pl.when((m == 1) & (group == 0))
                 def _():
                     take(up_s, 2)
                     issue(back_s, 0)
                     issue(back_s, 1)
-                    leave_out(0)
-                    mixed_save(0).start()
-                    enter_norm(0)
 
                 @pl.when((m == 1) & (group == 1))
                 def _():
@@ -1501,23 +1539,14 @@
             @pl.when(m == 0)
             def _():
                 reload_copy(3).start()
-                enter_out()
-                mid_g[1].relay()
-                cross(1, 0)
-                cross(1, 1)
+                take(up_s, 0)
+                issue(up_s, 2)
+
+            @pl.when(m == 0)
+            def _():
                 mid_g[1].finish()
                 for index in range(4):
                     reload_copy(index).wait()
-
-        leave_out(1)
-        mixed_save(1).start()
-        enter_norm(1)
-        token_load.wait()
-        saves = [mixed_save(m) for m in range(micro_count)]
-        down_s.finish(down_total)
-        saves.append(load(down_total, out_down))
-        gate_s.finish(gate_total)
-        saves.append(load(gate_total, out_gate))
 
         for half, norm_cols in enumerate((ky, val)):
 
@@ -1536,6 +1565,16 @@
         if outers > 1:
             for part in range(4):
                 issue(qkv_s, part)
+        leave_out(1)
+        mixed_save(1).start()
+        enter_norm(1)
+        token_load.wait()
+        saves = [mixed_save(m) for m in range(micro_count)]
+        down_s.finish(down_total)
+        saves.append(load(down_total, out_down))
+        gate_s.finish(gate_total)
+        saves.append(load(gate_total, out_gate))
+
         for part in range(3):
             take(back_s, part)
         leave_attn(0)
@@ -1721,22 +1760,38 @@
     buf_qkv,
     buf_back,
     buf_down,
+    turned_out,
+    turned_down,
     sems,
 ):
     flows = [
-        (in_qkv, buf_qkv, None),
-        (in_back, buf_back, None),
-        (in_down, buf_down, None),
-        (in_mixed, buf_mixed, mixed),
-        (in_tokens.at[0], buf_tokens.at[0], grad_tokens.at[0]),
-        (in_tokens.at[1], buf_tokens.at[1], grad_tokens.at[1]),
-        (in_gate, buf_gate, grad_gate),
-        (in_up, buf_up, grad_up),
+        (in_down, buf_down, ()),
+        (in_back, buf_back, ()),
+        (in_mixed, buf_mixed, ((buf_mixed, mixed),)),
+        (in_tokens.at[0], buf_tokens.at[0], ((buf_tokens.at[0], grad_tokens.at[0]),)),
+        (in_tokens.at[1], buf_tokens.at[1], ((buf_tokens.at[1], grad_tokens.at[1]),)),
+        (in_gate, buf_gate, ((buf_gate, grad_gate),)),
+        (in_up, buf_up, ((buf_up, grad_up),)),
+        (
+            in_qkv,
+            buf_qkv,
+            (
+                (buf_qkv.at[:, 0:256], grad_query),
+                (buf_qkv.at[:, 256:384], grad_key),
+                (buf_qkv.at[:, 384:512], grad_value),
+            ),
+        ),
     ]
     arrivals = [
         pltpu.make_async_copy(src, buf, sems.at[0, index]) for index, (src, buf, _) in enumerate(flows)
     ]
     departures = []
+
+    def depart(src, dst):
+        copy = pltpu.make_async_copy(src, dst, sems.at[1, len(departures)])
+        copy.start()
+        departures.append(copy)
+
     for copy in arrivals:
         copy.start()
     part = 0
@@ -1750,18 +1805,19 @@
         term = gains[part // 3 : part // 3 + 1, 128 * (part % 3) : 128 * (part % 3) + 128]
         out[...] = term[:, :DH] / gain[...] + term[:, DH:] / gain[...]
         part += 1
-    for index, (_, buf, dst) in enumerate(flows):
+    for index in range(2, len(flows)):
         arrivals[index].wait()
-        if dst is not None:
-            copy = pltpu.make_async_copy(buf, dst, sems.at[1, index])
-            copy.start()
-            departures.append(copy)
-        if index == 2:
-            grad_query[...] = buf_qkv[:, 0:256]
-            grad_key[...] = buf_qkv[:, 256:384]
-            grad_value[...] = buf_qkv[:, 384:512]
-            grad_out[...] = buf_back[...] if turned else buf_back[...].T
-            grad_down[...] = buf_down[...] if turned else buf_down[...].T
+        for src, dst in flows[index][2]:
+            depart(src, dst)
+    for index, (buf, facing, dst) in enumerate(
+        ((buf_down, turned_down, grad_down), (buf_back, turned_out, grad_out))
+    ):
+        arrivals[index].wait()
+        if turned:
+            depart(buf, dst)
+        else:
+            facing[...] = buf[...].T
+            depart(facing, dst)
     for copy in departures:
         copy.wait()
 
@@ -1797,7 +1853,7 @@
         functools.partial(deliver_kernel, turned),
         out_shape=out_shape,
         in_specs=[stored, stored] + [whole] * 3 + [stored] * 5,
-        out_specs=[anywhere, anywhere] + [whole] * 8 + [anywhere, anywhere, whole],
+        out_specs=[anywhere] * 2 + [whole] * 4 + [anywhere] * 7,
         scratch_shapes=[
             pltpu.VMEM(mixed.shape, BF16),
             pltpu.VMEM(grad_tokens.shape, F32),
@@ -1806,7 +1862,9 @@
             pltpu.VMEM(qkv.shape, F32),
             pltpu.VMEM(back.shape, F32),
             pltpu.VMEM(down.shape, F32),
-            pltpu.SemaphoreType.DMA((2, 8)),
+            pltpu.VMEM(facing(back), F32),
+            pltpu.VMEM(facing(down), F32),
+            pltpu.SemaphoreType.DMA((2, 16)),
         ],
         compiler_params=pltpu.CompilerParams(vmem_limit_bytes=VMEM_LIMIT),
         name="deliver_pass",

time: 258 us -> 246 us (0.953)
  Pallas kernels: 257 us -> 245 us
    pallas_call x1, Pallas kernels: 129 us -> 123 us  [backward(): pl.pallas_call(functools.partial(backward_kernel, dp_size), out_shape=out...]
    pallas_call x1, Pallas kernels: 123 us -> 117 us  [forward(): pl.pallas_call(functools.partial(forward_kernel, dp_size, turned), out_sh...]
where the time goes in v2:
time: 246 us
  Pallas kernels  245 us (100%)
    pallas_call x1, Pallas kernels, backward(): pl.pallas_call(functools.partial(backward_kernel, dp_size), out_shape=out...  123 us
    pallas_call x1, Pallas kernels, forward(): pl.pallas_call(functools.partial(forward_kernel, dp_size, turned), out_sh...  117 us
    pallas_call x1, Pallas kernels, deliver(): pl.pallas_call(functools.partial(deliver_kernel, turned), out_shape=out_s...  5.51 us

profile of v2, /device:TPU:0, one launch (start us, length us, event | category | flops | bytes accessed | tf_op | source)
XLA Modules:
  0.0 246.0 jit_solution(8952523847406237)
XLA Ops:
  0.6 117.1 %forward_pass.1 = (bf16[1024,512]{1,0:T(8,128)(2,1)}, bf16[1024,256]{1,0:T(8,128)(2,1)}, bf16[1024,1152]{1,0:T(8,128)(2,1)}, bf16[1024,1152]{1,0:T(8,128)(2,1)},...) custom-call(bf16[2,256,1024]{2,1,0:T(8,128)(2,1)} %bitcast.18, ...), custom_call_target="tpu_custom_call" | custom-call | tf_op jit(solution)/shard_map/forward_pass/pallas_call | solution.py:852
  117.8 122.5 %backward_pass.1 = (bf16[2,256,1024]{2,1,0:T(8,128)(2,1)}, f32[2,256,1024]{2,1,0:T(8,128)}, f32[8,384]{1,0:T(8,128)}, f32[128,512]{1,0:T(8,128)}, f32[128,256]{1...) custom-call(bf16[2,256,1024]{2,1,0:T(8,128)(2,1)} %bitcast.17, f32[1,1024]{1,0:T(1,128)} %bitcast.21, ...), custom_call_target="tpu_custom_call" | custom-call | tf_op jit(solution)/shard_map/backward_pass/pallas_call | solution.py:1718
  240.3 5.5 %deliver_pass.1 = (bf16[2,256,1024]{2,1,0:T(8,128)(2,1)}, f32[2,256,1024]{2,1,0:T(8,128)}, f32[1,1024]{1,0:T(1,128)}, f32[1,1024]{1,0:T(1,128)}, f32[1,64]{1,0:T...) custom-call(bf16[2,256,1024]{2,1,0:T(8,128)(2,1)} %get-tuple-element, ...), custom_call_target="tpu_custom_call" | custom-call | tf_op jit(solution)/shard_map/deliver_pass/pallas_call | solution.py:1852

commit v3 on v2

--- a/solution.py
+++ b/solution.py
@@ -432,11 +432,13 @@
         )
 
     saves = []
+    used = []
 
     def save(src, dst):
-        copy = pltpu.make_async_copy(src, dst, local_sems.at[len(saves)])
+        copy = pltpu.make_async_copy(src, dst, local_sems.at[len(used)])
         copy.start()
         saves.append(copy)
+        used.append(copy)
         return copy
 
     def save_columns(src, dst, m):
@@ -503,11 +505,13 @@
                     key_marks[head, m, rows] = jnp.where(chosen, 1.0, apart).astype(BF16)
         qkv_w.at(place.dp)[...] = qkv_shard[...]
         back_w.at(place.dp)[...] = back_shard[...]
-        gate_w.at(place.dp)[...] = gate_shard[...]
-        up_w.at(place.dp)[...] = up_shard[...]
-        for m in range(micro_count):
-            cot_all[m, own] = cotangent[m]
-
+
+    own_loads = [
+        save(gate_shard, gate_w.at(place.dp)),
+        save(up_shard, up_w.at(place.dp)),
+        save(cotangent.at[0], cot_all.at[0, own]),
+        save(cotangent.at[1], cot_all.at[1, own]),
+    ]
     prepare()
     save(down_shard, down_w.at(place.dp))
     save(tables, out_tables)
@@ -668,6 +672,9 @@
     enter_ffn(1)
     take(10)
     gate_w.finish()
+    for copy in own_loads:
+        saves.remove(copy)
+        copy.wait()
     save(gate_full, out_gate_full)
     take(11)
     down_w.begin()
@@ -730,6 +737,13 @@
             copy.start()
 
     save(hidden, out_hidden)
+
+    def down_copy(block):
+        rows = tile(block)
+        return pltpu.make_async_copy(
+            grad_down.at[rows], out_grad_down.at[rows], slope_sems.at[2 + block // 2, rem(block, 2)]
+        )
+
     for index in (tile_count - 2, tile_count - 1):
         for copy in slope_copies(index):
             copy.wait()
@@ -740,7 +754,10 @@
         columns = tile(block)
         grad_down[columns] = tn(cot_all[0, :, columns], hidden[0]).astype(BF16)
 
-    cot_g[1].relay()
+        @pl.when(block == block_count // 2)
+        def _():
+            cot_g[1].relay()
+
     cot_g[1].finish()
     save(cot_all.at[1], out_cot.at[1])
 
@@ -750,8 +767,8 @@
         grad_down[columns] = (
             grad_down[columns].astype(F32) + tn(cot_all[1, :, columns], hidden[1])
         ).astype(BF16)
-
-    save(grad_down, out_grad_down)
+        down_copy(block).start()
+
     down_w.finish()
     for piece in (qkv_w, back_w, gate_w, up_w, down_w):
         piece.drain()
@@ -760,6 +777,8 @@
         cot_g[m].drain()
         ffn_g[m].drain()
         branch_s(m).drain()
+    for block in range(block_count):
+        down_copy(block).wait()
     for copy in saves:
         copy.wait()
 
@@ -833,7 +852,7 @@
         pltpu.SemaphoreType.DMA((24,)),
         pltpu.SemaphoreType.DMA((24,)),
         pltpu.SemaphoreType.DMA((48,)),
-        pltpu.SemaphoreType.DMA((2, 2)),
+        pltpu.SemaphoreType.DMA((4, 2)),
     ]
     operands = (
         tokens,
@@ -852,7 +871,7 @@
     return pl.pallas_call(
         functools.partial(forward_kernel, dp_size, turned),
         out_shape=out_shape,
-        in_specs=[whole] * len(operands),
+        in_specs=[anywhere if index in (1, 7, 8) else whole for index in range(len(operands))],
         out_specs=[anywhere] * len(out_shape),
         scratch_shapes=scratch,
         compiler_params=pltpu.CompilerParams(
@@ -1243,7 +1262,10 @@
                 cols_copy(index + 1).start()
 
             ffn_w[kind, tile(block)] = (
-                tn(ffn_cols[slot, 0], grads[kind, 0]) + tn(ffn_cols[slot, 1], grads[kind, 1])
+                tn(
+                    ffn_cols[slot].reshape(micro_count * length, TILE),
+                    grads[kind].reshape(micro_count * length, hidden_width),
+                )
             ).astype(BF16)
 
             @pl.when(index == 1)
@@ -1557,7 +1579,10 @@
                     normed.at[turn_block(step)], norm_cols.at[slot], local_sems.at[24 + step]
                 ).wait()
                 qkv_part[tile(turn_block(step))] = (
-                    tn(norm_cols[slot, 0], grad_qkv[0]) + tn(norm_cols[slot, 1], grad_qkv[1])
+                    tn(
+                        norm_cols[slot].reshape(micro_count * length, TILE),
+                        grad_qkv[...].reshape(micro_count * length, 512),
+                    )
                 ).astype(BF16)
                 if outers == 1:
                     qkv_s.inner_copy(rem(step + 1, outer_size)).start()

time: 246 us -> 244 us (level)
  no operation moved by 1% of the time
where the time goes in v3:
time: 244 us
  Pallas kernels  243 us (100%)
    pallas_call x1, Pallas kernels, backward(): pl.pallas_call(functools.partial(backward_kernel, dp_size), out_shape=out...  123 us
    pallas_call x1, Pallas kernels, forward(): pl.pallas_call(functools.partial(forward_kernel, dp_size, turned), out_sh...  115 us
    pallas_call x1, Pallas kernels, deliver(): pl.pallas_call(functools.partial(deliver_kernel, turned), out_shape=out_s...  5.51 us

profile of v3, /device:TPU:0, one launch (start us, length us, event | category | flops | bytes accessed | tf_op | source)
XLA Modules:
  0.0 244.1 jit_solution(11146490769656013430)
XLA Ops:
  0.6 115.3 %forward_pass.1 = (bf16[1024,512]{1,0:T(8,128)(2,1)}, bf16[1024,256]{1,0:T(8,128)(2,1)}, bf16[1024,1152]{1,0:T(8,128)(2,1)}, bf16[1024,1152]{1,0:T(8,128)(2,1)},...) custom-call(bf16[2,256,1024]{2,1,0:T(8,128)(2,1)} %bitcast.18, ...), custom_call_target="tpu_custom_call" | custom-call | tf_op jit(solution)/shard_map/forward_pass/pallas_call | solution.py:871
  115.9 122.5 %backward_pass.1 = (bf16[2,256,1024]{2,1,0:T(8,128)(2,1)}, f32[2,256,1024]{2,1,0:T(8,128)}, f32[8,384]{1,0:T(8,128)}, f32[128,512]{1,0:T(8,128)}, f32[128,256]{1...) custom-call(bf16[2,256,1024]{2,1,0:T(8,128)(2,1)} %bitcast.17, f32[1,1024]{1,0:T(1,128)} %bitcast.21, ...), custom_call_target="tpu_custom_call" | custom-call | tf_op jit(solution)/shard_map/backward_pass/pallas_call | solution.py:1743
  238.4 5.5 %deliver_pass.1 = (bf16[2,256,1024]{2,1,0:T(8,128)(2,1)}, f32[2,256,1024]{2,1,0:T(8,128)}, f32[1,1024]{1,0:T(1,128)}, f32[1,1024]{1,0:T(1,128)}, f32[1,64]{1,0:T...) custom-call(bf16[2,256,1024]{2,1,0:T(8,128)(2,1)} %get-tuple-element, ...), custom_call_target="tpu_custom_call" | custom-call | tf_op jit(solution)/shard_map/deliver_pass/pallas_call | solution.py:1877
